TPU v7x, 128 devices: a whole 4x4x4 slice. The times are simulated.
128 devices in a mesh: ha: 4 (over z_lo, core), wa: 4 (over y), hd: 8 (over z_hi, x).
Axes of the slice: x: 4, y: 4, z: 4 (z_hi: 2, z_lo: 2; z = z_hi * 2 + z_lo), core: 2. Of those that a mesh axis runs over, the one named last changes fastest.
Arguments:
- queries: bfloat16 [12, 32, 64, 3072], P(None, 'ha', 'wa', 'hd'), may hold values from -10 to 10
- video_keys: bfloat16 [12, 32, 64, 3072], P(None, 'ha', 'wa', 'hd'), may hold values from -5 to 5
- video_values: bfloat16 [12, 32, 64, 3072], P(None, 'ha', 'wa', 'hd'), may hold values from -6 to 6
- text_keys: bfloat16 [256, 3072], P(None, 'hd'), may hold values from -5 to 5
- text_values: bfloat16 [256, 3072], P(None, 'hd'), may hold values from -6 to 6
- tile_radius: int32 [3, 2, 4, 8], P(None, None, 'ha', 'wa'), may hold values from 0 to 1, as said below
- out_weight: bfloat16 [3072, 3072], P('hd'), may hold values from -0.875 to 0.875
Outputs:
- projected: bfloat16 [12, 32, 64, 3072], P(None, 'ha', 'wa', 'hd')
Inputs may be any that keep to these rules, and one draw needn't show every extreme that they name: `tile_radius`: every video query has a window of at most one tile in each direction; some tile has radius 1 in all three.
All inputs are finite; a program needn't handle non-finite values.
Results may differ from a plain program's by a relative error of at most 0.012.
Values may be sent and summed in bfloat16 or wider, within the bound.
No kernel may reach another device: no remote copies, remote signals or barrier semaphores. Data moves between devices by JAX's collectives and lax.ppermute only.
A program may use at most 192 MiB of HBM per device.

v0:
```python
import functools
import jax
import jax.numpy as jnp
from jax import lax
from jax.experimental import pallas as pl
from jax.experimental.pallas import tpu as pltpu
from jax.sharding import PartitionSpec as P

HEAD=128; LIMIT=64.0
SCALE = 1.4426950408889634 * HEAD ** -0.5
NT=(((1,),(1,)),((),()))


def attend_kernel(rad, q, tk, tv, *refs, n_seg, coords, sub, times, split, QB):
    segs = refs[:n_seg]
    qs, kbuf, vbuf, tvb, mref, peak, acc, lst, cnt, sems = refs[-10:]
    out = refs[n_seg:-10]
    tiles = [(t, e) for t in times for e in range(2)]
    base = 6 * times[0]
    ha, wa, n_ha, n_wa = coords()
    copies=[]
    for i,s in enumerate(segs):
        copies.append(pltpu.make_async_copy(s.at[sub,0], kbuf.at[i], sems.at[2*i]))
        copies.append(pltpu.make_async_copy(s.at[sub,1], vbuf.at[i,:,pl.ds(0,128)], sems.at[2*i+1]))
    for c in copies: c.start()
    is_odd = ha % 2
    across_ok = jnp.where(is_odd==1, ha + 1 < n_ha, ha > 0).astype(jnp.int32)
    left_ok = (wa>0).astype(jnp.int32); right_ok=(wa+1<n_wa).astype(jnp.int32)
    rows=[0,0,1,1,2,2,0,0,1,1,2,2]
    cols=[0,1,0,1,0,1,-1,2,-1,2,-1,2]
    for qt, (t, e) in enumerate(tiles):
        r0=rad[0,t,0,e]; r1=rad[1,t,0,e]; r2=rad[2,t,0,e]
        row_ok=[1, (r1>=1).astype(jnp.int32), jnp.where(r1>=1, across_ok, 0)]
        n=jnp.int32(0)
        for s in range(12):
            gap=abs(cols[s]-e)
            if gap>1: continue
            ok=row_ok[rows[s]]
            if gap==1: ok=ok*(r2>=1).astype(jnp.int32)
            if cols[s]==-1: ok=ok*left_ok
            if cols[s]==2: ok=ok*right_ok
            place=s
            if s in (4,5): place=4+abs(s-4-is_odd)
            if s in (10,11): place=11-is_odd if s==10 else 10+is_odd
            lst[qt, n]=2*place+t
            n=n+ok
            lst[qt, n]=2*place+1-t
            n=n+ok*(r0>=1).astype(jnp.int32)
        cnt[qt]=n
    for qt, (t, e) in enumerate(tiles):
        f=6*t-base
        qs[qt]=q[f:f+6,:,8*e:8*e+8,:].reshape(384,HEAD)
    ones=jnp.ones((768,128),jnp.bfloat16)
    def fill(s,_):
        vbuf[s,:,128:256]=ones
        return 0
    lax.fori_loop(0,12,fill,0)
    tvb[:,0:128]=tv[...]
    tvb[:,128:256]=jnp.ones((256,128),jnp.bfloat16)

    def lanes_max(s):
        m=[s[:,128*j:128*j+128] for j in range(s.shape[1]//128)]
        while len(m)>1: m=[jnp.maximum(a,b) for a,b in zip(m[::2],m[1::2])]+([m[-1]] if len(m)%2 else [])
        return m[0]
    def bc(m, w):
        return jnp.concatenate([m]*(w//128),axis=1)
    def scores(qv,k):
        return lax.dot_general(qv,k,NT,preferred_element_type=jnp.float32)*SCALE
    def keys(code):
        return code//2, pl.ds(pl.multiple_of((code%2)*384,384),384)
    def text(qt,track):
        for r in range(0,384,QB):
            rs=pl.ds(r,QB)
            s=scores(qs[qt,rs,:],tk[...])
            if track:
                m=jnp.broadcast_to(jnp.max(s,axis=1,keepdims=True),(QB,128))
                mref[qt,rs,:]=m
                peak[qt,rs,:]=m
            else:
                m=mref[qt,rs,:]
            p=jnp.exp2(s-bc(m,256)).astype(jnp.bfloat16)
            acc[qt,rs,:]=jnp.dot(p,tvb[...],preferred_element_type=jnp.float32)
    def step(qt,codes):
        at=[keys(c) for c in codes]
        k=jnp.concatenate([kbuf[s,ks,:] for s,ks in at],axis=0)
        v=jnp.concatenate([vbuf[s,ks,:] for s,ks in at],axis=0)
        nxt=scores(qs[qt,pl.ds(0,QB),:],k)
        for r in range(0,384,QB):
            s=nxt
            if r+QB<384: nxt=scores(qs[qt,pl.ds(r+QB,QB),:],k)
            rs=pl.ds(r,QB)
            peak[qt,rs,:]=jnp.maximum(peak[qt,rs,:],lanes_max(s))
            p=jnp.exp2(s-bc(mref[qt,rs,:],s.shape[1])).astype(jnp.bfloat16)
            acc[qt,rs,:]+=jnp.dot(p,v,preferred_element_type=jnp.float32)
    for qt in range(len(tiles)):
        text(qt,True)
    for c in copies: c.wait()
    def one(qt,_):
        n=cnt[qt]
        def pair(i,_):
            step(qt,(lst[qt,2*i],lst[qt,2*i+1]))
            return 0
        lax.fori_loop(0,n//2,pair,0)
        @pl.when(n%2==1)
        def _():
            step(qt,(lst[qt,n-1],))
        return 0
    lax.fori_loop(0,len(tiles),one,0)
    gap=peak[0]-mref[0]
    for qt in range(1,len(tiles)): gap=jnp.maximum(gap,peak[qt]-mref[qt])
    @pl.when(jnp.max(gap)>LIMIT)
    def _():
        def redo(qt,_):
            text(qt,False)
            def safe(i,_):
                slot,ks=keys(lst[qt,i])
                def part(j,_):
                    rs=pl.ds(pl.multiple_of(j*128,128),128)
                    s=scores(qs[qt,rs,:],kbuf[slot,ks,:])
                    old=mref[qt,rs,:]
                    new=jnp.maximum(old,jnp.broadcast_to(jnp.max(s,axis=1,keepdims=True),(128,128)))
                    mref[qt,rs,:]=new
                    p=jnp.exp2(s-bc(new,384)).astype(jnp.bfloat16)
                    acc[qt,rs,:]=acc[qt,rs,:]*bc(jnp.exp2(old-new),256)+jnp.dot(p,vbuf[slot,ks,:],preferred_element_type=jnp.float32)
                    return 0
                return lax.fori_loop(0,3,part,0)
            return lax.fori_loop(0,cnt[qt],safe,0)
        lax.fori_loop(0,len(tiles),redo,0)
    for qt, (t, e) in enumerate(tiles):
        ref=out[times.index(t) if split else 0]
        f=0 if split else 6*t-base
        ref[f:f+6,:,8*e:8*e+8,:]=(acc[qt,:,0:128]/acc[qt,:,128:256]).astype(jnp.bfloat16).reshape(6,8,8,HEAD)


def attend(rad,q,tk,tv,segs,h,sub,coords,times=(0,1),split=True,QB=192):
    n=len(segs); nt=2*len(times); frames=6*len(times)
    first=times[0] if len(times)==1 else 0
    size=6 if split else frames
    return pl.pallas_call(
        functools.partial(attend_kernel,n_seg=n,coords=coords,sub=sub,times=times,split=split,QB=QB),
        grid=(1,),
        in_specs=[pl.BlockSpec(memory_space=pltpu.SMEM),
            pl.BlockSpec((frames,8,16,HEAD),lambda i:(first,0,0,h)),
            pl.BlockSpec((256,HEAD),lambda i:(0,h)),
            pl.BlockSpec((256,HEAD),lambda i:(0,h))]+[pl.BlockSpec(memory_space=pltpu.HBM)]*n,
        out_specs=[pl.BlockSpec((size,8,16,HEAD),lambda i:(0,0,0,0))]*(frames//size),
        out_shape=[jax.ShapeDtypeStruct((size,8,16,HEAD),jnp.bfloat16)]*(frames//size),
        scratch_shapes=[pltpu.VMEM((nt,384,HEAD),jnp.bfloat16),pltpu.VMEM((12,768,HEAD),jnp.bfloat16),
            pltpu.VMEM((12,768,256),jnp.bfloat16),pltpu.VMEM((256,256),jnp.bfloat16),
            pltpu.VMEM((nt,384,128),jnp.float32),pltpu.VMEM((nt,384,128),jnp.float32),pltpu.VMEM((nt,384,256),jnp.float32),
            pltpu.SMEM((nt,32),jnp.int32),pltpu.SMEM((nt,),jnp.int32),pltpu.SemaphoreType.DMA((2*n,))],
        cost_estimate=pl.CostEstimate(flops=3_000_000_000*len(times),transcendentals=6_000_000,bytes_accessed=6_000_000),
        name="attend",
    )(rad,q,tk,tv,*segs)


GROUPS = ((0, 1), (1, 2))


def pack_kernel(*refs):
    low, high = refs[-2:]
    for i in range(low.shape[0]):
        for col, ref in enumerate((low, high)):
            for j in range(2):
                ref[i, j] = refs[2 * i + j][:, :, 8 * col : 8 * col + 8, :]


def pack(keys, values, first, count):
    specs = [
        pl.BlockSpec((12, 8, 16, HEAD), lambda i, h=h: (0, 0, 0, h))
        for h in range(first, first + count)
        for _ in range(2)
    ]
    shape = (count, 2, 12, 8, 8, HEAD)
    outs = pl.pallas_call(
        pack_kernel,
        grid=(1,),
        in_specs=specs,
        out_specs=[pl.BlockSpec(shape, lambda i: (0,) * 6)] * 2,
        out_shape=[jax.ShapeDtypeStruct(shape, jnp.bfloat16)] * 2,
        cost_estimate=pl.CostEstimate(flops=500_000_000, transcendentals=0, bytes_accessed=1_600_000),
        name="pack",
    )(*[keys, values] * count)
    return [out.reshape(count, 2, 768, HEAD) for out in outs]


def choose_kernel(own_low, own_high, partner_low, partner_high, out, sem):
    ha = lax.axis_index("ha")
    inner = (ha > 0) & (ha + 1 < lax.axis_size("ha"))
    odd = ha % 2 == 1
    for is_inner, refs in ((True, (own_low, own_high)), (False, (partner_low, partner_high))):
        for is_odd, ref in enumerate(refs):

            @pl.when((inner == is_inner) & (odd == bool(is_odd)))
            def _():
                copy = pltpu.make_async_copy(ref, out, sem)
                copy.start()
                copy.wait()


def choose(*pieces):
    return pl.pallas_call(
        choose_kernel,
        in_specs=[pl.BlockSpec(memory_space=pltpu.HBM)] * 4,
        out_shape=jax.ShapeDtypeStruct(pieces[0].shape, jnp.bfloat16),
        scratch_shapes=[pltpu.SemaphoreType.DMA],
        cost_estimate=pl.CostEstimate(flops=200_000_000, transcendentals=0, bytes_accessed=800_000),
        name="choose",
    )(*pieces)


def cut_kernel(w, own, plus, minus, far):
    hd = lax.axis_index("hd")
    x = hd % 4
    plane = hd // 4
    for ref, step in ((own, 0), (plus, 1), (minus, 3), (far, 2)):
        for j in range(2):
            col = (x + step) % 4 + 4 * ((plane + j) % 2)
            ref[j] = w[:, pl.ds(pl.multiple_of(col * 384, 384), 384)]


def cut(weight):
    return pl.pallas_call(
        cut_kernel,
        out_shape=[jax.ShapeDtypeStruct((2, 384, 384), jnp.bfloat16)] * 4,
        cost_estimate=pl.CostEstimate(flops=500_000_000, transcendentals=0, bytes_accessed=4_800_000),
        name="cut",
    )(weight)


def product(refs, weights, a, b):
    @pl.when(pl.program_id(0) == 0)
    def _():
        for i in range(4):
            b[384 * i : 384 * (i + 1), :] = weights[i][0]

    for i in range(12):
        a[:, HEAD * i : HEAD * (i + 1)] = refs[i][...].reshape(256, HEAD)
    return jnp.dot(a[...], b[...], preferred_element_type=jnp.float32).reshape(2, 8, 16, 384)


def project_kernel(*refs):
    out, a, b = refs[16:]
    out[...] = product(refs, refs[12:16], a, b).astype(out.dtype)


def project(rows, weights, half, side, dtype):
    specs = [
        pl.BlockSpec((2, 8, 16, HEAD), lambda i, f=3 * half * (r.shape[0] // 12): (f + i, 0, 0, 0))
        for r in rows
    ]
    return pl.pallas_call(
        project_kernel,
        grid=(3,),
        in_specs=specs + [pl.BlockSpec((1, 384, 384), lambda i: (side, 0, 0))] * 4,
        out_specs=pl.BlockSpec((2, 8, 16, 384), lambda i: (i, 0, 0, 0)),
        out_shape=jax.ShapeDtypeStruct((6, 8, 16, 384), dtype),
        scratch_shapes=[pltpu.VMEM((256, 1536), jnp.bfloat16), pltpu.VMEM((1536, 384), jnp.bfloat16)],
        cost_estimate=pl.CostEstimate(flops=1_000_000_000, transcendentals=0, bytes_accessed=4_500_000),
        name="project",
    )(*rows, *weights)


def hd_pairs(step, planes=0):
    return [
        (4 * z + x, 4 * ((z + planes) % 2) + (x + step) % 4) for z in range(2) for x in range(4)
    ]


def place():
    return lax.axis_index("ha"), lax.axis_index("wa"), lax.axis_size("ha"), lax.axis_size("wa")


def shards(queries, video_keys, video_values, text_keys, text_values, tile_radius, out_weight):
    n_ha = lax.axis_size("ha")
    n_wa = lax.axis_size("wa")
    ring = [(i, (i + 1) % n_wa) for i in range(n_wa)]
    back = [(t, s) for s, t in ring]
    partner = [(i, i + 1 if i % 2 == 0 else i - 1) for i in range(n_ha)]
    chips = [(i, (i + 2) % n_ha) for i in range(n_ha)]
    turn = [
        (i * n_wa + s, i * n_wa + t)
        for i in range(n_ha)
        for s, t in (ring if i % 2 else back)
    ]

    def swap(piece):
        return lax.ppermute(piece, "ha", partner)

    windows = []
    for first, count in GROUPS:
        low, high = pack(video_keys, video_values, first, count)
        from_left = lax.ppermute(high, "wa", ring)
        from_right = lax.ppermute(low, "wa", back)
        partner_low, partner_high = swap(low), swap(high)
        picked = choose(low, high, partner_low, partner_high)
        over = lax.ppermute(picked, "ha", chips)
        corner = lax.ppermute(over, ("ha", "wa"), turn)
        window = (low, high, partner_low, partner_high, over, swap(over),
                  from_left, from_right, swap(from_left), swap(from_right),
                  corner, swap(corner))
        windows += [(window, i) for i in range(count)]
    pieces = cut(out_weight)
    weights = [
        pieces[0],
        lax.ppermute(pieces[1], "hd", hd_pairs(1)),
        lax.ppermute(pieces[2], "hd", hd_pairs(-1)),
        lax.ppermute(pieces[3], "hd", hd_pairs(2)),
    ]
    def spread(piece):
        return [
            piece,
            lax.ppermute(piece, "hd", hd_pairs(1)),
            lax.ppermute(piece, "hd", hd_pairs(-1)),
            lax.ppermute(piece, "hd", hd_pairs(2)),
        ]

    def head(h, times, split):
        window, sub = windows[h]
        return attend(tile_radius, queries, text_keys, text_values, window, h, sub, place, times, split)

    (whole,) = head(0, (0, 1), False)
    gathered = [[spread(whole)] * 2]
    halves = head(1, (0, 1), True)
    gathered.append([spread(halves[t]) for t in range(2)])
    last = {t: spread(head(2, (t,), True)[0]) for t in (1, 0)}
    gathered.append([last[0], last[1]])
    lines = [[gathered[h][t][g] for g in range(4) for h in range(3)] for t in range(2)]
    arrived = {}
    for t in (1, 0):
        other = project(lines[t], weights, t, 1, jnp.bfloat16)
        arrived[t] = lax.ppermute(other, "hd", hd_pairs(0, 1))
    outs = []
    for t in range(2):
        mine = project(lines[t], weights, t, 0, jnp.float32)
        outs.append((mine + arrived[t].astype(jnp.float32)).astype(jnp.bfloat16))
    return jnp.concatenate(outs, axis=0)


def solution(mesh):
    placed = (
        P(None, "ha", "wa", "hd"),
        P(None, "ha", "wa", "hd"),
        P(None, "ha", "wa", "hd"),
        P(None, "hd"),
        P(None, "hd"),
        P(None, None, "ha", "wa"),
        P("hd", None),
    )
    return jax.shard_map(
        shards, mesh=mesh, in_specs=placed, out_specs=P(None, "ha", "wa", "hd"), check_vma=False
    )
```

profile of v0, /device:TPU:120, one launch (start us, length us, event | category | flops | bytes accessed | tf_op | source)
XLA Modules:
  0.0 321.0 jit_solution(4733338050488141294)
XLA Ops:
  0.0 2.8 pack.3
  3.3 2.2 pack.2
  8.0 2.0 choose.3
  10.6 3.3 %cut.1 = (bf16[2,384,384]{2,1,0:T(8,128)(2,1)}, bf16[2,384,384]{2,1,0:T(8,128)(2,1)}, bf16[2,384,384]{2,1,0:T(8,128)(2,1)}, bf16[2,384,384]{2,1,0:T(8,128)(2,1)}) custom-call(bf16[384,3072]{1,0:T(8,128)(2,1)} %w.1), custom_call_target="tpu_custom_call" | custom-call | flops 500000000 | bytes 4800000 | tf_op jit(solution)/shard_map/cut/pallas_call | solution.py:223
  17.6 2.6 collective-permute-start.14
  22.6 5.7 %collective-permute-done.5.refs_7_ = bf16[1,2,768,128]{3,2,1,0:T(8,128)(2,1)} collective-permute-done((bf16[1,2,768,128]{3,2,1,0:T(8,128)(2,1)S(1)}, bf16[1,2,768,128]{3,2,1,0:T(8,128)(2,1)}, u32[]{:S(2)}, u32[]{:S(2)}) %collective-permute-start.5) | collective-permute-done | bytes 393248 | tf_op jit(solution)/shard_map/ppermute | solution.py:294
  30.3 1.8 collective-permute-start.15
  33.0 5.3 %collective-permute-done.2.refs_4_ = bf16[1,2,768,128]{3,2,1,0:T(8,128)(2,1)S(1)} collective-permute-done((bf16[1,2,768,128]{3,2,1,0:T(8,128)(2,1)}, bf16[1,2,768,128]{3,2,1,0:T(8,128)(2,1)S(1)}, u32[]{:S(2)}, u32[]{:S(2)}) %collective-permute-start.2) | collective-permute-done | bytes 393248 | tf_op jit(solution)/shard_map/ppermute | solution.py:297
  38.2 1.8 collective-permute-start.8
  40.6 22.2 %collective-permute-done.8.refs_10_ = bf16[1,2,768,128]{3,2,1,0:T(8,128)(2,1)} collective-permute-done((bf16[1,2,768,128]{3,2,1,0:T(8,128)(2,1)S(1)}, bf16[1,2,768,128]{3,2,1,0:T(8,128)(2,1)}, u32[]{:S(2)}, u32[]{:S(2)}) %collective-permute-start.8) | collective-permute-done | bytes 393248 | tf_op jit(solution)/shard_map/ppermute | solution.py:298
  68.1 66.0 %attend.4.refs_0_ = bf16[12,8,16,128]{3,2,1,0:T(8,128)(2,1)} custom-call(s32[3,2,1,2]{3,2,1,0:T(1,128)} %copy.8.rad, bf16[12,8,16,384]{3,2,1,0:T(8,128)(2,1)} %q.7, bf16[256,384]{1,0:T(8,128)(2,1)} %tk.7, bf16[256,384]{1,0:T(8,128)(2,1)} %tv.7, bf16[1,2,768,128]{3,2,1,0:T(8,128)(2,1)} %bitcast.18, bf16[1,2,768,128]{3,2,1,0:T(8,128)(2,1)} %bitcast.23, ...), custom_call_target="tpu_custom_call" | custom-call | flops 6000000000 | bytes 6000000 | tf_op jit(solution)/shard_map/attend/pallas_call | solution.py:139
  134.1 2.8 collective-permute-start.26
  139.0 66.0 %attend.5 = (bf16[6,8,16,128]{3,2,1,0:T(8,128)(2,1)}, bf16[6,8,16,128]{3,2,1,0:T(8,128)(2,1)}) custom-call(s32[3,2,1,2]{3,2,1,0:T(1,128)} %copy.8.rad, bf16[12,8,16,384]{3,2,1,0:T(8,128)(2,1)} %q.7, bf16[256,384]{1,0:T(8,128)(2,1)} %tk.7, bf16[256,384]{1,0:T(8,128)(2,1)} %tv.7, bf16[2,2,768,128]{3,2,1,0:T(8,128)(2,1)} %bitcast.6, ...), custom_call_target="tpu_custom_call" | custom-call | flops 6000000000 | bytes 6000000 | tf_op jit(solution)/shard_map/attend/pallas_call | solution.py:139
  205.9 2.3 collective-permute-start.24
  208.1 24.3 %attend.6.refs_2_ = bf16[6,8,16,128]{3,2,1,0:T(8,128)(2,1)} custom-call(s32[3,2,1,2]{3,2,1,0:T(1,128)} %copy.8.rad, bf16[12,8,16,384]{3,2,1,0:T(8,128)(2,1)} %q.7, bf16[256,384]{1,0:T(8,128)(2,1)} %tk.7, bf16[256,384]{1,0:T(8,128)(2,1)} %tv.7, bf16[2,2,768,128]{3,2,1,0:T(8,128)(2,1)} %bitcast.7, bf16[2,2,768,128]{3,2,1,0:T(8,128)(2,1)} %bitcast.13, ...), custom_call_target="tpu_custom_call" | custom-call | flops 3000000000 | bytes 6000000 | tf_op jit(solution)/shard_map/attend/pallas_call | solution.py:139
  232.5 2.4 collective-permute-start.37
  234.9 2.0 collective-permute-start.35
  240.7 46.1 %attend.7.refs_2_ = bf16[6,8,16,128]{3,2,1,0:T(8,128)(2,1)} custom-call(s32[3,2,1,2]{3,2,1,0:T(1,128)} %copy.8.rad, bf16[12,8,16,384]{3,2,1,0:T(8,128)(2,1)} %q.7, bf16[256,384]{1,0:T(8,128)(2,1)} %tk.7, bf16[256,384]{1,0:T(8,128)(2,1)} %tv.7, bf16[2,2,768,128]{3,2,1,0:T(8,128)(2,1)} %bitcast.8, bf16[2,2,768,128]{3,2,1,0:T(8,128)(2,1)} %bitcast.14, ...), custom_call_target="tpu_custom_call" | custom-call | flops 3000000000 | bytes 6000000 | tf_op jit(solution)/shard_map/attend/pallas_call | solution.py:139
  287.0 3.6 %collective-permute-start.38 = (bf16[6,8,16,128]{3,2,1,0:T(8,128)(2,1)}, bf16[6,8,16,128]{3,2,1,0:T(8,128)(2,1)S(1)}, u32[]{:S(2)}, u32[]{:S(2)}) collective-permute-start(bf16[6,8,16,128]{3,2,1,0:T(8,128)(2,1)} %attend.7.refs_2_), channel_id=1, source_target_pairs={{0,2},{1,3},{2,0},{3,1},{4,6},{5,7},{6,4},{7,5},{8,10},{9,11},{10,... | collective-permute-start | bytes 589832 | tf_op jit(solution)/shard_map/ppermute | solution.py:315
  292.6 4.9 %project.5 = bf16[6,8,16,384]{3,2,1,0:T(8,128)(2,1)} custom-call(bf16[12,8,16,128]{3,2,1,0:T(8,128)(2,1)} %attend.4.refs_0_, bf16[6,8,16,128]{3,2,1,0:T(8,128)(2,1)} %get-tuple-element.19.refs_1_, bf16[6,8,16,128]{3,2,1,0:T(8,128)(2,1)} %attend.6.refs_2_, bf16[12,8,16,128]{3,2,1,0:T(8,128)(2,1)} %copy-done.5, bf16[6,8,16,128]{3,2,1,0:T(8,128)(2,1)} %copy-done.10, ...), custom_call_target="tpu_custom_call" | custom-call | flops 1000000000 | bytes 4500000 | tf_op jit(solution)/shard_map/project/pallas_call | solution.py:252
  299.9 4.9 %project.7 = bf16[6,8,16,384]{3,2,1,0:T(8,128)(2,1)} custom-call(bf16[12,8,16,128]{3,2,1,0:T(8,128)(2,1)} %attend.4.refs_0_, bf16[6,8,16,128]{3,2,1,0:T(8,128)(2,1)} %get-tuple-element.24.refs_1_, bf16[6,8,16,128]{3,2,1,0:T(8,128)(2,1)} %attend.7.refs_2_, bf16[12,8,16,128]{3,2,1,0:T(8,128)(2,1)} %copy-done.5, bf16[6,8,16,128]{3,2,1,0:T(8,128)(2,1)} %copy-done.16, ...), custom_call_target="tpu_custom_call" | custom-call | flops 1000000000 | bytes 4500000 | tf_op jit(solution)/shard_map/project/pallas_call | solution.py:252
  304.8 3.1 collective-permute-start.39
  307.9 5.0 %project.6 = f32[6,8,16,384]{3,2,1,0:T(8,128)} custom-call(bf16[12,8,16,128]{3,2,1,0:T(8,128)(2,1)} %attend.4.refs_0_, bf16[6,8,16,128]{3,2,1,0:T(8,128)(2,1)} %get-tuple-element.24.refs_1_, bf16[6,8,16,128]{3,2,1,0:T(8,128)(2,1)} %attend.7.refs_2_, bf16[12,8,16,128]{3,2,1,0:T(8,128)(2,1)} %copy-done.5, bf16[6,8,16,128]{3,2,1,0:T(8,128)(2,1)} %copy-done.16, ...), custom_call_target="tpu_custom_call" | custom-call | flops 1000000000 | bytes 4500000 | tf_op jit(solution)/shard_map/project/pallas_call | solution.py:252
  313.0 5.1 %project.4 = f32[6,8,16,384]{3,2,1,0:T(8,128)} custom-call(bf16[12,8,16,128]{3,2,1,0:T(8,128)(2,1)} %attend.4.refs_0_, bf16[6,8,16,128]{3,2,1,0:T(8,128)(2,1)} %get-tuple-element.19.refs_1_, bf16[6,8,16,128]{3,2,1,0:T(8,128)(2,1)} %attend.6.refs_2_, bf16[12,8,16,128]{3,2,1,0:T(8,128)(2,1)} %copy-done.5, bf16[6,8,16,128]{3,2,1,0:T(8,128)(2,1)} %copy-done.10, ...), custom_call_target="tpu_custom_call" | custom-call | flops 1000000000 | bytes 4500000 | tf_op jit(solution)/shard_map/project/pallas_call | solution.py:252
  (139 shorter events, 32.5 us)
Async XLA Ops:
  10.1 22.1 %collective-permute-start.12 = (bf16[2,2,768,128]{3,2,1,0:T(8,128)(2,1)}, bf16[2,2,768,128]{3,2,1,0:T(8,128)(2,1)}, u32[]{:S(2)}, u32[]{:S(2)}) collective-permute-start(bf16[2,2,768,128]{3,2,1,0:T(8,128)(2,1)} %choose.3), channel_id=1, source_target_pairs={{0,64},{32,96},{64,0},{96,32},{1,65},{33,97},{65,1},{97,33},{2,66}... | collective-permute-start | bytes 2359304 | tf_op jit(solution)/shard_map/ppermute | solution.py:297
  17.6 22.5 %collective-permute-start.14 = (bf16[2,2,768,128]{3,2,1,0:T(8,128)(2,1)S(1)}, bf16[2,2,768,128]{3,2,1,0:T(8,128)(2,1)}, u32[]{:S(2)}, u32[]{:S(2)}) collective-permute-start(bf16[2,2,768,128]{3,2,1,0:T(8,128)(2,1)S(1)} %bitcast.15), channel_id=1, source_target_pairs={{0,8},{8,16},{16,24},{24,0},{1,9},{9,17},{17,25},{25,1},{2,10},{10... | collective-permute-start | bytes 2359304 | tf_op jit(solution)/shard_map/ppermute | solution.py:293
  30.3 32.4 %collective-permute-start.15 = (bf16[2,2,768,128]{3,2,1,0:T(8,128)(2,1)S(1)}, bf16[2,2,768,128]{3,2,1,0:T(8,128)(2,1)}, u32[]{:S(2)}, u32[]{:S(2)}) collective-permute-start(bf16[2,2,768,128]{3,2,1,0:T(8,128)(2,1)S(1)} %bitcast.9), channel_id=1, source_target_pairs={{8,0},{16,8},{24,16},{0,24},{9,1},{17,9},{25,17},{1,25},{10,2},{18... | collective-permute-start | bytes 2359304 | tf_op jit(solution)/shard_map/ppermute | solution.py:294
  32.2 31.2 %collective-permute-start.18 = (bf16[2,2,768,128]{3,2,1,0:T(8,128)(2,1)}, bf16[2,2,768,128]{3,2,1,0:T(8,128)(2,1)}, u32[]{:S(2)}, u32[]{:S(2)}) collective-permute-start(bf16[2,2,768,128]{3,2,1,0:T(8,128)(2,1)} %collective-permute-done.12.refs_4_), channel_id=1, source_target_pairs={{8,0},{16,8},{24,16},{0,24},{32,40},{40,48},{48,56},{56,32},{72,64... | collective-permute-start | bytes 2359304 | tf_op jit(solution)/shard_map/ppermute | solution.py:298
  38.2 24.5 %collective-permute-start.8 = (bf16[1,2,768,128]{3,2,1,0:T(8,128)(2,1)S(1)}, bf16[1,2,768,128]{3,2,1,0:T(8,128)(2,1)}, u32[]{:S(2)}, u32[]{:S(2)}) collective-permute-start(bf16[1,2,768,128]{3,2,1,0:T(8,128)(2,1)S(1)} %collective-permute-done.2.refs_4_), channel_id=1, source_target_pairs={{8,0},{16,8},{24,16},{0,24},{32,40},{40,48},{48,56},{56,32},{72,64... | collective-permute-start | bytes 1179656 | tf_op jit(solution)/shard_map/ppermute | solution.py:298
  40.0 26.4 %collective-permute-start.16 = (bf16[2,2,768,128]{3,2,1,0:T(8,128)(2,1)}, bf16[2,2,768,128]{3,2,1,0:T(8,128)(2,1)S(1)}, u32[]{:S(2)}, u32[]{:S(2)}) collective-permute-start(bf16[2,2,768,128]{3,2,1,0:T(8,128)(2,1)} %collective-permute-done.14.refs_6_), channel_id=1, source_target_pairs={{0,32},{32,0},{64,96},{96,64},{1,33},{33,1},{65,97},{97,65},{2,34}... | collective-permute-start | bytes 2359304 | tf_op jit(solution)/shard_map/ppermute | solution.py:288
  40.1 23.2 %collective-permute-start.3 = (bf16[1,2,768,128]{3,2,1,0:T(8,128)(2,1)S(1)}, bf16[1,2,768,128]{3,2,1,0:T(8,128)(2,1)S(1)}, u32[]{:S(2)}, u32[]{:S(2)}) collective-permute-start(bf16[1,2,768,128]{3,2,1,0:T(8,128)(2,1)S(1)} %collective-permute-done.2.refs_4_), channel_id=1, source_target_pairs={{0,32},{32,0},{64,96},{96,64},{1,33},{33,1},{65,97},{97,65},{2,34}... | collective-permute-start | bytes 1179656 | tf_op jit(solution)/shard_map/ppermute | solution.py:288
  62.7 71.4 %collective-permute-start.17 = (bf16[2,2,768,128]{3,2,1,0:T(8,128)(2,1)}, bf16[2,2,768,128]{3,2,1,0:T(8,128)(2,1)S(1)}, u32[]{:S(2)}, u32[]{:S(2)}) collective-permute-start(bf16[2,2,768,128]{3,2,1,0:T(8,128)(2,1)} %collective-permute-done.15.refs_7_), channel_id=1, source_target_pairs={{0,32},{32,0},{64,96},{96,64},{1,33},{33,1},{65,97},{97,65},{2,34}... | collective-permute-start | bytes 2359304 | tf_op jit(solution)/shard_map/ppermute | solution.py:288
  63.2 73.7 %collective-permute-start.13 = (bf16[2,2,768,128]{3,2,1,0:T(8,128)(2,1)}, bf16[2,2,768,128]{3,2,1,0:T(8,128)(2,1)}, u32[]{:S(2)}, u32[]{:S(2)}) collective-permute-start(bf16[2,2,768,128]{3,2,1,0:T(8,128)(2,1)} %collective-permute-done.12.refs_4_), channel_id=1, source_target_pairs={{0,32},{32,0},{64,96},{96,64},{1,33},{33,1},{65,97},{97,65},{2,34}... | collective-permute-start | bytes 2359304 | tf_op jit(solution)/shard_map/ppermute | solution.py:288
  63.3 74.4 %collective-permute-start.19 = (bf16[2,2,768,128]{3,2,1,0:T(8,128)(2,1)}, bf16[2,2,768,128]{3,2,1,0:T(8,128)(2,1)}, u32[]{:S(2)}, u32[]{:S(2)}) collective-permute-start(bf16[2,2,768,128]{3,2,1,0:T(8,128)(2,1)} %collective-permute-done.18.refs_10_), channel_id=1, source_target_pairs={{0,32},{32,0},{64,96},{96,64},{1,33},{33,1},{65,97},{97,65},{2,34}... | collective-permute-start | bytes 2359304 | tf_op jit(solution)/shard_map/ppermute | solution.py:288
  64.8 140.2 %collective-permute-start.30 = (bf16[2,384,384]{2,1,0:T(8,128)(2,1)}, bf16[2,384,384]{2,1,0:T(8,128)(2,1)S(1)}, u32[]{:S(2)}, u32[]{:S(2)}) collective-permute-start(bf16[2,384,384]{2,1,0:T(8,128)(2,1)} %get-tuple-element.22), channel_id=1, source_target_pairs={{0,3},{1,0},{2,1},{3,2},{4,7},{5,4},{6,5},{7,6},{8,11},{9,8},{10,9... | collective-permute-start | bytes 1769480 | tf_op jit(solution)/shard_map/ppermute | solution.py:307
  67.3 138.5 %collective-permute-start.31 = (bf16[2,384,384]{2,1,0:T(8,128)(2,1)}, bf16[2,384,384]{2,1,0:T(8,128)(2,1)S(1)}, u32[]{:S(2)}, u32[]{:S(2)}) collective-permute-start(bf16[2,384,384]{2,1,0:T(8,128)(2,1)} %get-tuple-element.23), channel_id=1, source_target_pairs={{0,2},{1,3},{2,0},{3,1},{4,6},{5,7},{6,4},{7,5},{8,10},{9,11},{10,... | collective-permute-start | bytes 1769480 | tf_op jit(solution)/shard_map/ppermute | solution.py:308
  134.1 74.0 %collective-permute-start.26 = (bf16[12,8,16,128]{3,2,1,0:T(8,128)(2,1)}, bf16[12,8,16,128]{3,2,1,0:T(8,128)(2,1)S(1)}, u32[]{:S(2)}, u32[]{:S(2)}) collective-permute-start(bf16[12,8,16,128]{3,2,1,0:T(8,128)(2,1)} %attend.4.refs_0_), channel_id=1, source_target_pairs={{0,2},{1,3},{2,0},{3,1},{4,6},{5,7},{6,4},{7,5},{8,10},{9,11},{10,... | collective-permute-start | bytes 1179656 | tf_op jit(solution)/shard_map/ppermute | solution.py:315
  136.9 95.6 %collective-permute-start.23 = (bf16[12,8,16,128]{3,2,1,0:T(8,128)(2,1)}, bf16[12,8,16,128]{3,2,1,0:T(8,128)(2,1)S(1)}, u32[]{:S(2)}, u32[]{:S(2)}) collective-permute-start(bf16[12,8,16,128]{3,2,1,0:T(8,128)(2,1)} %attend.4.refs_0_), channel_id=1, source_target_pairs={{0,3},{1,0},{2,1},{3,2},{4,7},{5,4},{6,5},{7,6},{8,11},{9,8},{10,9... | collective-permute-start | bytes 1179656 | tf_op jit(solution)/shard_map/ppermute | solution.py:314
  137.8 97.2 %collective-permute-start.20 = (bf16[12,8,16,128]{3,2,1,0:T(8,128)(2,1)}, bf16[12,8,16,128]{3,2,1,0:T(8,128)(2,1)S(1)}, u32[]{:S(2)}, u32[]{:S(2)}) collective-permute-start(bf16[12,8,16,128]{3,2,1,0:T(8,128)(2,1)} %attend.4.refs_0_), channel_id=1, source_target_pairs={{0,1},{1,2},{2,3},{3,0},{4,5},{5,6},{6,7},{7,4},{8,9},{9,10},{10,1... | collective-permute-start | bytes 1179656 | tf_op jit(solution)/shard_map/ppermute | solution.py:313
  205.0 32.0 %collective-permute-start.27 = (bf16[6,8,16,128]{3,2,1,0:T(8,128)(2,1)}, bf16[6,8,16,128]{3,2,1,0:T(8,128)(2,1)S(1)}, u32[]{:S(2)}, u32[]{:S(2)}) collective-permute-start(bf16[6,8,16,128]{3,2,1,0:T(8,128)(2,1)} %get-tuple-element.19.refs_1_), channel_id=1, source_target_pairs={{0,2},{1,3},{2,0},{3,1},{4,6},{5,7},{6,4},{7,5},{8,10},{9,11},{10,... | collective-permute-start | bytes 589832 | tf_op jit(solution)/shard_map/ppermute | solution.py:315
  205.9 32.7 %collective-permute-start.24 = (bf16[6,8,16,128]{3,2,1,0:T(8,128)(2,1)}, bf16[6,8,16,128]{3,2,1,0:T(8,128)(2,1)S(1)}, u32[]{:S(2)}, u32[]{:S(2)}) collective-permute-start(bf16[6,8,16,128]{3,2,1,0:T(8,128)(2,1)} %get-tuple-element.19.refs_1_), channel_id=1, source_target_pairs={{0,3},{1,0},{2,1},{3,2},{4,7},{5,4},{6,5},{7,6},{8,11},{9,8},{10,9... | collective-permute-start | bytes 589832 | tf_op jit(solution)/shard_map/ppermute | solution.py:314
  208.1 31.5 %collective-permute-start.21 = (bf16[6,8,16,128]{3,2,1,0:T(8,128)(2,1)}, bf16[6,8,16,128]{3,2,1,0:T(8,128)(2,1)S(1)}, u32[]{:S(2)}, u32[]{:S(2)}) collective-permute-start(bf16[6,8,16,128]{3,2,1,0:T(8,128)(2,1)} %get-tuple-element.19.refs_1_), channel_id=1, source_target_pairs={{0,1},{1,2},{2,3},{3,0},{4,5},{5,6},{6,7},{7,4},{8,9},{9,10},{10,1... | collective-permute-start | bytes 589832 | tf_op jit(solution)/shard_map/ppermute | solution.py:313
  232.5 54.3 %collective-permute-start.37 = (bf16[6,8,16,128]{3,2,1,0:T(8,128)(2,1)S(1)}, bf16[6,8,16,128]{3,2,1,0:T(8,128)(2,1)S(1)}, u32[]{:S(2)}, u32[]{:S(2)}) collective-permute-start(bf16[6,8,16,128]{3,2,1,0:T(8,128)(2,1)S(1)} %copy-done.9), channel_id=1, source_target_pairs={{0,2},{1,3},{2,0},{3,1},{4,6},{5,7},{6,4},{7,5},{8,10},{9,11},{10,... | collective-permute-start | bytes 589832 | tf_op jit(solution)/shard_map/ppermute | solution.py:315
  234.9 62.6 %collective-permute-start.35 = (bf16[6,8,16,128]{3,2,1,0:T(8,128)(2,1)S(1)}, bf16[6,8,16,128]{3,2,1,0:T(8,128)(2,1)S(1)}, u32[]{:S(2)}, u32[]{:S(2)}) collective-permute-start(bf16[6,8,16,128]{3,2,1,0:T(8,128)(2,1)S(1)} %copy-done.9), channel_id=1, source_target_pairs={{0,3},{1,0},{2,1},{3,2},{4,7},{5,4},{6,5},{7,6},{8,11},{9,8},{10,9... | collective-permute-start | bytes 589832 | tf_op jit(solution)/shard_map/ppermute | solution.py:314
  237.0 50.0 %collective-permute-start.28 = (bf16[6,8,16,128]{3,2,1,0:T(8,128)(2,1)}, bf16[6,8,16,128]{3,2,1,0:T(8,128)(2,1)S(1)}, u32[]{:S(2)}, u32[]{:S(2)}) collective-permute-start(bf16[6,8,16,128]{3,2,1,0:T(8,128)(2,1)} %attend.6.refs_2_), channel_id=1, source_target_pairs={{0,2},{1,3},{2,0},{3,1},{4,6},{5,7},{6,4},{7,5},{8,10},{9,11},{10,... | collective-permute-start | bytes 589832 | tf_op jit(solution)/shard_map/ppermute | solution.py:315
  238.6 52.0 %collective-permute-start.25 = (bf16[6,8,16,128]{3,2,1,0:T(8,128)(2,1)}, bf16[6,8,16,128]{3,2,1,0:T(8,128)(2,1)S(1)}, u32[]{:S(2)}, u32[]{:S(2)}) collective-permute-start(bf16[6,8,16,128]{3,2,1,0:T(8,128)(2,1)} %attend.6.refs_2_), channel_id=1, source_target_pairs={{0,3},{1,0},{2,1},{3,2},{4,7},{5,4},{6,5},{7,6},{8,11},{9,8},{10,9... | collective-permute-start | bytes 589832 | tf_op jit(solution)/shard_map/ppermute | solution.py:314
  239.7 51.7 %collective-permute-start.22 = (bf16[6,8,16,128]{3,2,1,0:T(8,128)(2,1)}, bf16[6,8,16,128]{3,2,1,0:T(8,128)(2,1)S(1)}, u32[]{:S(2)}, u32[]{:S(2)}) collective-permute-start(bf16[6,8,16,128]{3,2,1,0:T(8,128)(2,1)} %attend.6.refs_2_), channel_id=1, source_target_pairs={{0,1},{1,2},{2,3},{3,0},{4,5},{5,6},{6,7},{7,4},{8,9},{9,10},{10,1... | collective-permute-start | bytes 589832 | tf_op jit(solution)/shard_map/ppermute | solution.py:313
  297.6 20.5 %collective-permute-start.32 = (bf16[6,8,16,384]{3,2,1,0:T(8,128)(2,1)}, bf16[6,8,16,384]{3,2,1,0:T(8,128)(2,1)S(1)}, u32[]{:S(2)}, u32[]{:S(2)}) collective-permute-start(bf16[6,8,16,384]{3,2,1,0:T(8,128)(2,1)} %project.5), channel_id=1, source_target_pairs={{0,4},{1,5},{2,6},{3,7},{4,0},{5,1},{6,2},{7,3},{8,12},{9,13},{10,... | collective-permute-start | bytes 1769480 | tf_op jit(solution)/shard_map/ppermute | solution.py:332
  (49 other events, 788.3 us)
where the time goes:
time: 322 us; the launch traced here: 321 us
  Pallas kernels  234 us (73%)
  starting transfers between devices  41.2 us (13%)
  waiting for transfers between devices  36.8 us (11%)
  local copies, waits for them, and re-layouts  5.46 us (2%)
    pallas_call x4, Pallas kernels, attend(): pl.pallas_call(functools.partial(attend_kernel, n_seg=n, coords=coords, s...  202 us
    ppermute x2, waiting for transfers between devices, shards(): corner = lax.ppermute(over, ('ha', 'wa'), turn)  22.2 us
    pallas_call x4, Pallas kernels, project(): pl.pallas_call(project_kernel, grid=(3,), in_specs=specs + [pl.BlockSpec(...  19.9 us
    ppermute x5, starting transfers between devices, spread(): lax.ppermute(piece, 'hd', hd_pairs(2))  11.4 us
    ppermute x5, starting transfers between devices, spread(): lax.ppermute(piece, 'hd', hd_pairs(-1))  6.95 us
  transfers between devices with their start and end apart: 40, of which 8 were waited for; matrix products, arithmetic and copies ran while one was open for 1% of the time, Pallas kernels for 72%

commit v1 on v0

--- a/solution.py
+++ b/solution.py
@@ -155,6 +155,7 @@
 
 
 GROUPS = ((0, 1), (1, 2))
+STEPS = 1
 
 
 def pack_kernel(*refs):
@@ -235,8 +236,8 @@
             b[384 * i : 384 * (i + 1), :] = weights[i][0]
 
     for i in range(12):
-        a[:, HEAD * i : HEAD * (i + 1)] = refs[i][...].reshape(256, HEAD)
-    return jnp.dot(a[...], b[...], preferred_element_type=jnp.float32).reshape(2, 8, 16, 384)
+        a[:, HEAD * i : HEAD * (i + 1)] = refs[i][...].reshape(-1, HEAD)
+    return jnp.dot(a[...], b[...], preferred_element_type=jnp.float32).reshape(-1, 8, 16, 384)
 
 
 def project_kernel(*refs):
@@ -244,18 +245,19 @@
     out[...] = product(refs, refs[12:16], a, b).astype(out.dtype)
 
 
-def project(rows, weights, half, side, dtype):
+def project(rows, weights, half, side, dtype, steps=STEPS):
+    size = 6 // steps
     specs = [
-        pl.BlockSpec((2, 8, 16, HEAD), lambda i, f=3 * half * (r.shape[0] // 12): (f + i, 0, 0, 0))
+        pl.BlockSpec((size, 8, 16, HEAD), lambda i, f=steps * half * (r.shape[0] // 12): (f + i, 0, 0, 0))
         for r in rows
     ]
     return pl.pallas_call(
         project_kernel,
-        grid=(3,),
+        grid=(steps,),
         in_specs=specs + [pl.BlockSpec((1, 384, 384), lambda i: (side, 0, 0))] * 4,
-        out_specs=pl.BlockSpec((2, 8, 16, 384), lambda i: (i, 0, 0, 0)),
+        out_specs=pl.BlockSpec((size, 8, 16, 384), lambda i: (i, 0, 0, 0)),
         out_shape=jax.ShapeDtypeStruct((6, 8, 16, 384), dtype),
-        scratch_shapes=[pltpu.VMEM((256, 1536), jnp.bfloat16), pltpu.VMEM((1536, 384), jnp.bfloat16)],
+        scratch_shapes=[pltpu.VMEM((128 * size, 1536), jnp.bfloat16), pltpu.VMEM((1536, 384), jnp.bfloat16)],
         cost_estimate=pl.CostEstimate(flops=1_000_000_000, transcendentals=0, bytes_accessed=4_500_000),
         name="project",
     )(*rows, *weights)
@@ -272,6 +274,7 @@
 
 
 def shards(queries, video_keys, video_values, text_keys, text_values, tile_radius, out_weight):
+    n_frames = queries.shape[0]
     n_ha = lax.axis_size("ha")
     n_wa = lax.axis_size("wa")
     ring = [(i, (i + 1) % n_wa) for i in range(n_wa)]
@@ -319,22 +322,22 @@
         window, sub = windows[h]
         return attend(tile_radius, queries, text_keys, text_values, window, h, sub, place, times, split)
 
-    (whole,) = head(0, (0, 1), False)
-    gathered = [[spread(whole)] * 2]
-    halves = head(1, (0, 1), True)
-    gathered.append([spread(halves[t]) for t in range(2)])
-    last = {t: spread(head(2, (t,), True)[0]) for t in (1, 0)}
-    gathered.append([last[0], last[1]])
+    (first_head,) = head(0, (0, 1), False)
+    (second_head,) = head(1, (0, 1), False)
+    halves = head(2, (0, 1), True)
+    last = {t: spread(halves[t]) for t in (1, 0)}
+    gathered = [[spread(first_head)] * 2, [spread(second_head)] * 2, [last[0], last[1]]]
     lines = [[gathered[h][t][g] for g in range(4) for h in range(3)] for t in range(2)]
     arrived = {}
     for t in (1, 0):
         other = project(lines[t], weights, t, 1, jnp.bfloat16)
         arrived[t] = lax.ppermute(other, "hd", hd_pairs(0, 1))
-    outs = []
-    for t in range(2):
+    done = {}
+    for t in (1, 0):
         mine = project(lines[t], weights, t, 0, jnp.float32)
-        outs.append((mine + arrived[t].astype(jnp.float32)).astype(jnp.bfloat16))
-    return jnp.concatenate(outs, axis=0)
+        done[t] = (mine + arrived[t].astype(jnp.float32)).astype(jnp.bfloat16)
+    out = jnp.pad(done[1], ((n_frames // 2, 0), (0, 0), (0, 0), (0, 0)))
+    return lax.dynamic_update_slice(out, done[0], (0, 0, 0, 0))
 
 
 def solution(mesh):

time: 322 us -> 338 us (1.050)
  the two profiles are of different devices: /device:TPU:120 before, /device:TPU:52 now
where the time goes in v1:
time: 338 us
  Pallas kernels  248 us (73%)
  waiting for transfers between devices  44.6 us (13%)
  starting transfers between devices  36.7 us (11%)
  local copies, waits for them, and re-layouts  6.31 us (2%)
    pallas_call x3, Pallas kernels, attend(): pl.pallas_call(functools.partial(attend_kernel, n_seg=n, coords=coords, s...  218 us
    pallas_call x4, Pallas kernels, project(): pl.pallas_call(project_kernel, grid=(steps,), in_specs=specs + [pl.BlockS...  17.9 us
    ppermute x2, waiting for transfers between devices, shards(): over = lax.ppermute(picked, 'ha', chips)  14.9 us
    ppermute x2, waiting for transfers between devices, shards(): corner = lax.ppermute(over, ('ha', 'wa'), turn)  14.7 us
    ppermute x4, starting transfers between devices, spread(): lax.ppermute(piece, 'hd', hd_pairs(2))  10.7 us
    ppermute x4, waiting for transfers between devices, spread(): lax.ppermute(piece, 'hd', hd_pairs(-1))  7.62 us
  transfers between devices with their start and end apart: 37, of which 8 were waited for; matrix products, arithmetic and copies ran while one was open for 0% of the time, Pallas kernels for 73%

profile of v1, /device:TPU:52, one launch (start us, length us, event | category | flops | bytes accessed | tf_op | source)
XLA Modules:
  0.0 337.6 jit_solution(13141152237390615230)
XLA Ops:
  0.0 2.8 pack.3
  3.3 2.2 pack.2
  7.8 2.0 choose.3
  13.7 1.8 choose.2
  15.5 2.0 collective-permute-start.2
  17.4 3.7 %collective-permute-done.4.refs_6_ = bf16[1,2,768,128]{3,2,1,0:T(8,128)(2,1)S(1)} collective-permute-done((bf16[1,2,768,128]{3,2,1,0:T(8,128)(2,1)S(1)}, bf16[1,2,768,128]{3,2,1,0:T(8,128)(2,1)S(1)}, u32[]{:S(2)}, u32[]{:S(2)}) %collective-permute-start.4) | collective-permute-done | bytes 393248 | tf_op jit(solution)/shard_map/ppermute | solution.py:296
  23.3 14.9 %collective-permute-done.2.refs_4_ = bf16[1,2,768,128]{3,2,1,0:T(8,128)(2,1)S(1)} collective-permute-done((bf16[1,2,768,128]{3,2,1,0:T(8,128)(2,1)}, bf16[1,2,768,128]{3,2,1,0:T(8,128)(2,1)S(1)}, u32[]{:S(2)}, u32[]{:S(2)}) %collective-permute-start.2) | collective-permute-done | bytes 393248 | tf_op jit(solution)/shard_map/ppermute | solution.py:300
  40.2 14.7 %collective-permute-done.8.refs_10_ = bf16[1,2,768,128]{3,2,1,0:T(8,128)(2,1)} collective-permute-done((bf16[1,2,768,128]{3,2,1,0:T(8,128)(2,1)S(1)}, bf16[1,2,768,128]{3,2,1,0:T(8,128)(2,1)}, u32[]{:S(2)}, u32[]{:S(2)}) %collective-permute-start.8) | collective-permute-done | bytes 393248 | tf_op jit(solution)/shard_map/ppermute | solution.py:301
  57.4 3.3 cut.1
  62.0 72.7 %attend.3.refs_0_ = bf16[12,8,16,128]{3,2,1,0:T(8,128)(2,1)} custom-call(s32[3,2,1,2]{3,2,1,0:T(1,128)} %copy.8.rad, bf16[12,8,16,384]{3,2,1,0:T(8,128)(2,1)} %q.5, bf16[256,384]{1,0:T(8,128)(2,1)} %tk.5, bf16[256,384]{1,0:T(8,128)(2,1)} %tv.5, bf16[1,2,768,128]{3,2,1,0:T(8,128)(2,1)} %bitcast.16, bf16[1,2,768,128]{3,2,1,0:T(8,128)(2,1)} %bitcast.20, ...), custom_call_target="tpu_custom_call" | custom-call | flops 6000000000 | bytes 6000000 | tf_op jit(solution)/shard_map/attend/pallas_call | solution.py:139
  135.7 1.8 collective-permute-start.31
  139.5 72.7 %attend.4.refs_1_ = bf16[12,8,16,128]{3,2,1,0:T(8,128)(2,1)} custom-call(s32[3,2,1,2]{3,2,1,0:T(1,128)} %copy.8.rad, bf16[12,8,16,384]{3,2,1,0:T(8,128)(2,1)} %q.5, bf16[256,384]{1,0:T(8,128)(2,1)} %tk.5, bf16[256,384]{1,0:T(8,128)(2,1)} %tv.5, bf16[2,2,768,128]{3,2,1,0:T(8,128)(2,1)} %bitcast.6, bf16[2,2,768,128]{3,2,1,0:T(8,128)(2,1)} %bitcast.11, ...), custom_call_target="tpu_custom_call" | custom-call | flops 6000000000 | bytes 6000000 | tf_op jit(solution)/shard_map/attend/pallas_call | solution.py:139
  212.3 3.1 collective-permute-start.26
  215.4 72.7 %attend.5 = (bf16[6,8,16,128]{3,2,1,0:T(8,128)(2,1)}, bf16[6,8,16,128]{3,2,1,0:T(8,128)(2,1)}) custom-call(s32[3,2,1,2]{3,2,1,0:T(1,128)} %copy.8.rad, bf16[12,8,16,384]{3,2,1,0:T(8,128)(2,1)} %q.5, bf16[256,384]{1,0:T(8,128)(2,1)} %tk.5, bf16[256,384]{1,0:T(8,128)(2,1)} %tv.5, bf16[2,2,768,128]{3,2,1,0:T(8,128)(2,1)} %bitcast.7, ...), custom_call_target="tpu_custom_call" | custom-call | flops 6000000000 | bytes 6000000 | tf_op jit(solution)/shard_map/attend/pallas_call | solution.py:139
  290.4 2.2 collective-permute-start.27
  294.1 2.4 collective-permute-start.35
  296.5 7.6 %collective-permute-done.34.refs_8_ = bf16[6,8,16,128]{3,2,1,0:T(8,128)(2,1)S(1)} collective-permute-done((bf16[6,8,16,128]{3,2,1,0:T(8,128)(2,1)}, bf16[6,8,16,128]{3,2,1,0:T(8,128)(2,1)S(1)}, u32[]{:S(2)}, u32[]{:S(2)}) %collective-permute-start.34) | collective-permute-done | bytes 196640 | tf_op jit(solution)/shard_map/ppermute | solution.py:317
  305.8 1.9 collective-permute-start.25
  307.7 3.0 collective-permute-start.28
  312.3 4.4 %project.7 = bf16[6,8,16,384]{3,2,1,0:T(8,128)(2,1)} custom-call(bf16[12,8,16,128]{3,2,1,0:T(8,128)(2,1)} %attend.3.refs_0_, bf16[12,8,16,128]{3,2,1,0:T(8,128)(2,1)} %attend.4.refs_1_, bf16[6,8,16,128]{3,2,1,0:T(8,128)(2,1)} %get-tuple-element.24.refs_2_, bf16[12,8,16,128]{3,2,1,0:T(8,128)(2,1)} %copy-done.4, bf16[12,8,16,128]{3,2,1,0:T(8,128)(2,1)} %copy-done.7, ...), custom_call_target="tpu_custom_call" | custom-call | flops 1000000000 | bytes 4500000 | tf_op jit(solution)/shard_map/project/pallas_call | solution.py:254
  316.6 3.0 collective-permute-start.36
  320.4 4.3 %project.5 = bf16[6,8,16,384]{3,2,1,0:T(8,128)(2,1)} custom-call(bf16[12,8,16,128]{3,2,1,0:T(8,128)(2,1)} %attend.3.refs_0_, bf16[12,8,16,128]{3,2,1,0:T(8,128)(2,1)} %attend.4.refs_1_, bf16[6,8,16,128]{3,2,1,0:T(8,128)(2,1)} %get-tuple-element.19.refs_2_, bf16[12,8,16,128]{3,2,1,0:T(8,128)(2,1)} %copy-done.4, bf16[12,8,16,128]{3,2,1,0:T(8,128)(2,1)} %copy-done.7, ...), custom_call_target="tpu_custom_call" | custom-call | flops 1000000000 | bytes 4500000 | tf_op jit(solution)/shard_map/project/pallas_call | solution.py:254
  325.3 4.6 %project.6 = f32[6,8,16,384]{3,2,1,0:T(8,128)} custom-call(bf16[12,8,16,128]{3,2,1,0:T(8,128)(2,1)} %attend.3.refs_0_, bf16[12,8,16,128]{3,2,1,0:T(8,128)(2,1)} %attend.4.refs_1_, bf16[6,8,16,128]{3,2,1,0:T(8,128)(2,1)} %get-tuple-element.24.refs_2_, bf16[12,8,16,128]{3,2,1,0:T(8,128)(2,1)} %copy-done.4, bf16[12,8,16,128]{3,2,1,0:T(8,128)(2,1)} %copy-done.7, ...), custom_call_target="tpu_custom_call" | custom-call | flops 1000000000 | bytes 4500000 | tf_op jit(solution)/shard_map/project/pallas_call | solution.py:254
  329.8 4.7 %project.4 = f32[6,8,16,384]{3,2,1,0:T(8,128)} custom-call(bf16[12,8,16,128]{3,2,1,0:T(8,128)(2,1)} %attend.3.refs_0_, bf16[12,8,16,128]{3,2,1,0:T(8,128)(2,1)} %attend.4.refs_1_, bf16[6,8,16,128]{3,2,1,0:T(8,128)(2,1)} %get-tuple-element.19.refs_2_, bf16[12,8,16,128]{3,2,1,0:T(8,128)(2,1)} %copy-done.4, bf16[12,8,16,128]{3,2,1,0:T(8,128)(2,1)} %copy-done.7, ...), custom_call_target="tpu_custom_call" | custom-call | flops 1000000000 | bytes 4500000 | tf_op jit(solution)/shard_map/project/pallas_call | solution.py:254
  (132 shorter events, 28.9 us)
Async XLA Ops:
  9.9 28.3 %collective-permute-start.12 = (bf16[2,2,768,128]{3,2,1,0:T(8,128)(2,1)}, bf16[2,2,768,128]{3,2,1,0:T(8,128)(2,1)}, u32[]{:S(2)}, u32[]{:S(2)}) collective-permute-start(bf16[2,2,768,128]{3,2,1,0:T(8,128)(2,1)} %choose.3), channel_id=1, source_target_pairs={{0,64},{32,96},{64,0},{96,32},{1,65},{33,97},{65,1},{97,33},{2,66}... | collective-permute-start | bytes 2359304 | tf_op jit(solution)/shard_map/ppermute | solution.py:300
  15.5 22.7 %collective-permute-start.2 = (bf16[1,2,768,128]{3,2,1,0:T(8,128)(2,1)}, bf16[1,2,768,128]{3,2,1,0:T(8,128)(2,1)S(1)}, u32[]{:S(2)}, u32[]{:S(2)}) collective-permute-start(bf16[1,2,768,128]{3,2,1,0:T(8,128)(2,1)} %choose.2), channel_id=1, source_target_pairs={{0,64},{32,96},{64,0},{96,32},{1,65},{33,97},{65,1},{97,33},{2,66}... | collective-permute-start | bytes 1179656 | tf_op jit(solution)/shard_map/ppermute | solution.py:300
  21.2 17.5 %collective-permute-start.6 = (bf16[1,2,768,128]{3,2,1,0:T(8,128)(2,1)S(1)}, bf16[1,2,768,128]{3,2,1,0:T(8,128)(2,1)S(1)}, u32[]{:S(2)}, u32[]{:S(2)}) collective-permute-start(bf16[1,2,768,128]{3,2,1,0:T(8,128)(2,1)S(1)} %collective-permute-done.4.refs_6_), channel_id=1, source_target_pairs={{0,32},{32,0},{64,96},{96,64},{1,33},{33,1},{65,97},{97,65},{2,34}... | collective-permute-start | bytes 1179656 | tf_op jit(solution)/shard_map/ppermute | solution.py:291
  21.2 33.7 %collective-permute-start.14 = (bf16[2,2,768,128]{3,2,1,0:T(8,128)(2,1)S(1)}, bf16[2,2,768,128]{3,2,1,0:T(8,128)(2,1)}, u32[]{:S(2)}, u32[]{:S(2)}) collective-permute-start(bf16[2,2,768,128]{3,2,1,0:T(8,128)(2,1)S(1)} %bitcast.13), channel_id=1, source_target_pairs={{0,8},{8,16},{16,24},{24,0},{1,9},{9,17},{17,25},{25,1},{2,10},{10... | collective-permute-start | bytes 2359304 | tf_op jit(solution)/shard_map/ppermute | solution.py:296
  22.5 32.9 %collective-permute-start.15 = (bf16[2,2,768,128]{3,2,1,0:T(8,128)(2,1)S(1)}, bf16[2,2,768,128]{3,2,1,0:T(8,128)(2,1)S(1)}, u32[]{:S(2)}, u32[]{:S(2)}) collective-permute-start(bf16[2,2,768,128]{3,2,1,0:T(8,128)(2,1)S(1)} %bitcast.8), channel_id=1, source_target_pairs={{8,0},{16,8},{24,16},{0,24},{9,1},{17,9},{25,17},{1,25},{10,2},{18... | collective-permute-start | bytes 2359304 | tf_op jit(solution)/shard_map/ppermute | solution.py:297
  38.2 18.2 %collective-permute-start.18 = (bf16[2,2,768,128]{3,2,1,0:T(8,128)(2,1)}, bf16[2,2,768,128]{3,2,1,0:T(8,128)(2,1)}, u32[]{:S(2)}, u32[]{:S(2)}) collective-permute-start(bf16[2,2,768,128]{3,2,1,0:T(8,128)(2,1)} %collective-permute-done.12.refs_4_), channel_id=1, source_target_pairs={{8,0},{16,8},{24,16},{0,24},{32,40},{40,48},{48,56},{56,32},{72,64... | collective-permute-start | bytes 2359304 | tf_op jit(solution)/shard_map/ppermute | solution.py:301
  38.7 16.2 %collective-permute-start.8 = (bf16[1,2,768,128]{3,2,1,0:T(8,128)(2,1)S(1)}, bf16[1,2,768,128]{3,2,1,0:T(8,128)(2,1)}, u32[]{:S(2)}, u32[]{:S(2)}) collective-permute-start(bf16[1,2,768,128]{3,2,1,0:T(8,128)(2,1)S(1)} %collective-permute-done.2.refs_4_), channel_id=1, source_target_pairs={{8,0},{16,8},{24,16},{0,24},{32,40},{40,48},{48,56},{56,32},{72,64... | collective-permute-start | bytes 1179656 | tf_op jit(solution)/shard_map/ppermute | solution.py:301
  40.1 15.4 %collective-permute-start.3 = (bf16[1,2,768,128]{3,2,1,0:T(8,128)(2,1)S(1)}, bf16[1,2,768,128]{3,2,1,0:T(8,128)(2,1)S(1)}, u32[]{:S(2)}, u32[]{:S(2)}) collective-permute-start(bf16[1,2,768,128]{3,2,1,0:T(8,128)(2,1)S(1)} %collective-permute-done.2.refs_4_), channel_id=1, source_target_pairs={{0,32},{32,0},{64,96},{96,64},{1,33},{33,1},{65,97},{97,65},{2,34}... | collective-permute-start | bytes 1179656 | tf_op jit(solution)/shard_map/ppermute | solution.py:291
  54.9 79.8 %collective-permute-start.16 = (bf16[2,2,768,128]{3,2,1,0:T(8,128)(2,1)}, bf16[2,2,768,128]{3,2,1,0:T(8,128)(2,1)S(1)}, u32[]{:S(2)}, u32[]{:S(2)}) collective-permute-start(bf16[2,2,768,128]{3,2,1,0:T(8,128)(2,1)} %collective-permute-done.14.refs_6_), channel_id=1, source_target_pairs={{0,32},{32,0},{64,96},{96,64},{1,33},{33,1},{65,97},{97,65},{2,34}... | collective-permute-start | bytes 2359304 | tf_op jit(solution)/shard_map/ppermute | solution.py:291
  55.4 80.2 %collective-permute-start.17 = (bf16[2,2,768,128]{3,2,1,0:T(8,128)(2,1)S(1)}, bf16[2,2,768,128]{3,2,1,0:T(8,128)(2,1)}, u32[]{:S(2)}, u32[]{:S(2)}) collective-permute-start(bf16[2,2,768,128]{3,2,1,0:T(8,128)(2,1)S(1)} %collective-permute-done.15.refs_7_), channel_id=1, source_target_pairs={{0,32},{32,0},{64,96},{96,64},{1,33},{33,1},{65,97},{97,65},{2,34}... | collective-permute-start | bytes 2359304 | tf_op jit(solution)/shard_map/ppermute | solution.py:291
  55.5 81.9 %collective-permute-start.13 = (bf16[2,2,768,128]{3,2,1,0:T(8,128)(2,1)}, bf16[2,2,768,128]{3,2,1,0:T(8,128)(2,1)}, u32[]{:S(2)}, u32[]{:S(2)}) collective-permute-start(bf16[2,2,768,128]{3,2,1,0:T(8,128)(2,1)} %collective-permute-done.12.refs_4_), channel_id=1, source_target_pairs={{0,32},{32,0},{64,96},{96,64},{1,33},{33,1},{65,97},{97,65},{2,34}... | collective-permute-start | bytes 2359304 | tf_op jit(solution)/shard_map/ppermute | solution.py:291
  56.4 82.2 %collective-permute-start.19 = (bf16[2,2,768,128]{3,2,1,0:T(8,128)(2,1)}, bf16[2,2,768,128]{3,2,1,0:T(8,128)(2,1)}, u32[]{:S(2)}, u32[]{:S(2)}) collective-permute-start(bf16[2,2,768,128]{3,2,1,0:T(8,128)(2,1)} %collective-permute-done.18.refs_10_), channel_id=1, source_target_pairs={{0,32},{32,0},{64,96},{96,64},{1,33},{33,1},{65,97},{97,65},{2,34}... | collective-permute-start | bytes 2359304 | tf_op jit(solution)/shard_map/ppermute | solution.py:291
  60.7 151.5 %collective-permute-start.29 = (bf16[2,384,384]{2,1,0:T(8,128)(2,1)}, bf16[2,384,384]{2,1,0:T(8,128)(2,1)S(1)}, u32[]{:S(2)}, u32[]{:S(2)}) collective-permute-start(bf16[2,384,384]{2,1,0:T(8,128)(2,1)} %get-tuple-element.21), channel_id=1, source_target_pairs={{0,1},{1,2},{2,3},{3,0},{4,5},{5,6},{6,7},{7,4},{8,9},{9,10},{10,1... | collective-permute-start | bytes 1769480 | tf_op jit(solution)/shard_map/ppermute | solution.py:309
  134.8 153.4 %collective-permute-start.30 = (bf16[2,384,384]{2,1,0:T(8,128)(2,1)}, bf16[2,384,384]{2,1,0:T(8,128)(2,1)S(1)}, u32[]{:S(2)}, u32[]{:S(2)}) collective-permute-start(bf16[2,384,384]{2,1,0:T(8,128)(2,1)} %get-tuple-element.22), channel_id=1, source_target_pairs={{0,3},{1,0},{2,1},{3,2},{4,7},{5,4},{6,5},{7,6},{8,11},{9,8},{10,9... | collective-permute-start | bytes 1769480 | tf_op jit(solution)/shard_map/ppermute | solution.py:310
  135.7 152.5 %collective-permute-start.31 = (bf16[2,384,384]{2,1,0:T(8,128)(2,1)}, bf16[2,384,384]{2,1,0:T(8,128)(2,1)S(1)}, u32[]{:S(2)}, u32[]{:S(2)}) collective-permute-start(bf16[2,384,384]{2,1,0:T(8,128)(2,1)} %get-tuple-element.23), channel_id=1, source_target_pairs={{0,2},{1,3},{2,0},{3,1},{4,6},{5,7},{6,4},{7,5},{8,10},{9,11},{10,... | collective-permute-start | bytes 1769480 | tf_op jit(solution)/shard_map/ppermute | solution.py:311
  137.4 152.5 %collective-permute-start.20 = (bf16[12,8,16,128]{3,2,1,0:T(8,128)(2,1)}, bf16[12,8,16,128]{3,2,1,0:T(8,128)(2,1)S(1)}, u32[]{:S(2)}, u32[]{:S(2)}) collective-permute-start(bf16[12,8,16,128]{3,2,1,0:T(8,128)(2,1)} %attend.3.refs_0_), channel_id=1, source_target_pairs={{0,1},{1,2},{2,3},{3,0},{4,5},{5,6},{6,7},{7,4},{8,9},{9,10},{10,1... | collective-permute-start | bytes 1179656 | tf_op jit(solution)/shard_map/ppermute | solution.py:316
  138.6 151.8 %collective-permute-start.23 = (bf16[12,8,16,128]{3,2,1,0:T(8,128)(2,1)}, bf16[12,8,16,128]{3,2,1,0:T(8,128)(2,1)S(1)}, u32[]{:S(2)}, u32[]{:S(2)}) collective-permute-start(bf16[12,8,16,128]{3,2,1,0:T(8,128)(2,1)} %attend.3.refs_0_), channel_id=1, source_target_pairs={{0,3},{1,0},{2,1},{3,2},{4,7},{5,4},{6,5},{7,6},{8,11},{9,8},{10,9... | collective-permute-start | bytes 1179656 | tf_op jit(solution)/shard_map/ppermute | solution.py:317
  212.3 80.3 %collective-permute-start.26 = (bf16[12,8,16,128]{3,2,1,0:T(8,128)(2,1)S(1)}, bf16[12,8,16,128]{3,2,1,0:T(8,128)(2,1)}, u32[]{:S(2)}, u32[]{:S(2)}) collective-permute-start(bf16[12,8,16,128]{3,2,1,0:T(8,128)(2,1)S(1)} %copy-done.3), channel_id=1, source_target_pairs={{0,2},{1,3},{2,0},{3,1},{4,6},{5,7},{6,4},{7,5},{8,10},{9,11},{10,... | collective-permute-start | bytes 1179656 | tf_op jit(solution)/shard_map/ppermute | solution.py:318
  288.3 19.4 %collective-permute-start.21 = (bf16[12,8,16,128]{3,2,1,0:T(8,128)(2,1)S(1)}, bf16[12,8,16,128]{3,2,1,0:T(8,128)(2,1)S(1)}, u32[]{:S(2)}, u32[]{:S(2)}) collective-permute-start(bf16[12,8,16,128]{3,2,1,0:T(8,128)(2,1)S(1)} %copy-done.6), channel_id=1, source_target_pairs={{0,1},{1,2},{2,3},{3,0},{4,5},{5,6},{6,7},{7,4},{8,9},{9,10},{10,1... | collective-permute-start | bytes 1179656 | tf_op jit(solution)/shard_map/ppermute | solution.py:316
  290.0 20.7 %collective-permute-start.24 = (bf16[12,8,16,128]{3,2,1,0:T(8,128)(2,1)S(1)}, bf16[12,8,16,128]{3,2,1,0:T(8,128)(2,1)S(1)}, u32[]{:S(2)}, u32[]{:S(2)}) collective-permute-start(bf16[12,8,16,128]{3,2,1,0:T(8,128)(2,1)S(1)} %copy-done.6), channel_id=1, source_target_pairs={{0,3},{1,0},{2,1},{3,2},{4,7},{5,4},{6,5},{7,6},{8,11},{9,8},{10,9... | collective-permute-start | bytes 1179656 | tf_op jit(solution)/shard_map/ppermute | solution.py:317
  290.4 20.3 %collective-permute-start.27 = (bf16[12,8,16,128]{3,2,1,0:T(8,128)(2,1)S(1)}, bf16[12,8,16,128]{3,2,1,0:T(8,128)(2,1)S(1)}, u32[]{:S(2)}, u32[]{:S(2)}) collective-permute-start(bf16[12,8,16,128]{3,2,1,0:T(8,128)(2,1)S(1)} %copy-done.6), channel_id=1, source_target_pairs={{0,2},{1,3},{2,0},{3,1},{4,6},{5,7},{6,4},{7,5},{8,10},{9,11},{10,... | collective-permute-start | bytes 1179656 | tf_op jit(solution)/shard_map/ppermute | solution.py:318
  304.1 15.5 %collective-permute-start.22 = (bf16[6,8,16,128]{3,2,1,0:T(8,128)(2,1)}, bf16[6,8,16,128]{3,2,1,0:T(8,128)(2,1)S(1)}, u32[]{:S(2)}, u32[]{:S(2)}) collective-permute-start(bf16[6,8,16,128]{3,2,1,0:T(8,128)(2,1)} %get-tuple-element.19.refs_2_), channel_id=1, source_target_pairs={{0,1},{1,2},{2,3},{3,0},{4,5},{5,6},{6,7},{7,4},{8,9},{9,10},{10,1... | collective-permute-start | bytes 589832 | tf_op jit(solution)/shard_map/ppermute | solution.py:316
  305.8 13.8 %collective-permute-start.25 = (bf16[6,8,16,128]{3,2,1,0:T(8,128)(2,1)}, bf16[6,8,16,128]{3,2,1,0:T(8,128)(2,1)S(1)}, u32[]{:S(2)}, u32[]{:S(2)}) collective-permute-start(bf16[6,8,16,128]{3,2,1,0:T(8,128)(2,1)} %get-tuple-element.19.refs_2_), channel_id=1, source_target_pairs={{0,3},{1,0},{2,1},{3,2},{4,7},{5,4},{6,5},{7,6},{8,11},{9,8},{10,9... | collective-permute-start | bytes 589832 | tf_op jit(solution)/shard_map/ppermute | solution.py:317
  316.6 17.9 %collective-permute-start.36 = (bf16[6,8,16,384]{3,2,1,0:T(8,128)(2,1)}, bf16[6,8,16,384]{3,2,1,0:T(8,128)(2,1)S(1)}, u32[]{:S(2)}, u32[]{:S(2)}) collective-permute-start(bf16[6,8,16,384]{3,2,1,0:T(8,128)(2,1)} %project.7), channel_id=1, source_target_pairs={{0,4},{1,5},{2,6},{3,7},{4,0},{5,1},{6,2},{7,3},{8,12},{9,13},{10,... | collective-permute-start | bytes 1769480 | tf_op jit(solution)/shard_map/ppermute | solution.py:334
  (46 other events, 659.9 us)

commit v2 on v1

--- a/solution.py
+++ b/solution.py
@@ -11,7 +11,7 @@
 NT=(((1,),(1,)),((),()))
 
 
-def attend_kernel(rad, q, tk, tv, *refs, n_seg, coords, sub, times, split, QB):
+def attend_kernel(rad, q, tk, tv, *refs, n_seg, coords, sub, times, split, QB, KW):
     segs = refs[:n_seg]
     qs, kbuf, vbuf, tvb, mref, peak, acc, lst, cnt, sems = refs[-10:]
     out = refs[n_seg:-10]
@@ -84,23 +84,30 @@
         at=[keys(c) for c in codes]
         k=jnp.concatenate([kbuf[s,ks,:] for s,ks in at],axis=0)
         v=jnp.concatenate([vbuf[s,ks,:] for s,ks in at],axis=0)
-        nxt=scores(qs[qt,pl.ds(0,QB),:],k)
-        for r in range(0,384,QB):
+        W=min(KW,k.shape[0]) if k.shape[0]%KW==0 else k.shape[0]
+        parts=[(r,c) for r in range(0,384,QB) for c in range(0,k.shape[0],W)]
+        def part(r,c): return scores(qs[qt,pl.ds(r,QB),:],k[c:c+W])
+        nxt=part(*parts[0])
+        for i,(r,c) in enumerate(parts):
             s=nxt
-            if r+QB<384: nxt=scores(qs[qt,pl.ds(r+QB,QB),:],k)
+            if i+1<len(parts): nxt=part(*parts[i+1])
             rs=pl.ds(r,QB)
             peak[qt,rs,:]=jnp.maximum(peak[qt,rs,:],lanes_max(s))
             p=jnp.exp2(s-bc(mref[qt,rs,:],s.shape[1])).astype(jnp.bfloat16)
-            acc[qt,rs,:]+=jnp.dot(p,v,preferred_element_type=jnp.float32)
+            acc[qt,rs,:]+=jnp.dot(p,v[c:c+W],preferred_element_type=jnp.float32)
     for qt in range(len(tiles)):
         text(qt,True)
     for c in copies: c.wait()
     def one(qt,_):
         n=cnt[qt]
-        def pair(i,_):
-            step(qt,(lst[qt,2*i],lst[qt,2*i+1]))
+        def quad(i,_):
+            step(qt,[lst[qt,4*i+j] for j in range(4)])
             return 0
-        lax.fori_loop(0,n//2,pair,0)
+        lax.fori_loop(0,n//4,quad,0)
+        m=n//4*4
+        @pl.when(n%4>=2)
+        def _():
+            step(qt,(lst[qt,m],lst[qt,m+1]))
         @pl.when(n%2==1)
         def _():
             step(qt,(lst[qt,n-1],))
@@ -132,12 +139,12 @@
         ref[f:f+6,:,8*e:8*e+8,:]=(acc[qt,:,0:128]/acc[qt,:,128:256]).astype(jnp.bfloat16).reshape(6,8,8,HEAD)
 
 
-def attend(rad,q,tk,tv,segs,h,sub,coords,times=(0,1),split=True,QB=192):
+def attend(rad,q,tk,tv,segs,h,sub,coords,times=(0,1),split=True,QB=192,KW=768):
     n=len(segs); nt=2*len(times); frames=6*len(times)
     first=times[0] if len(times)==1 else 0
     size=6 if split else frames
     return pl.pallas_call(
-        functools.partial(attend_kernel,n_seg=n,coords=coords,sub=sub,times=times,split=split,QB=QB),
+        functools.partial(attend_kernel,n_seg=n,coords=coords,sub=sub,times=times,split=split,QB=QB,KW=KW),
         grid=(1,),
         in_specs=[pl.BlockSpec(memory_space=pltpu.SMEM),
             pl.BlockSpec((frames,8,16,HEAD),lambda i:(first,0,0,h)),

time: 338 us -> 334 us (0.988)
  the two profiles are of different devices: /device:TPU:52 before, /device:TPU:48 now
where the time goes in v2:
time: 334 us
  Pallas kernels  244 us (73%)
  waiting for transfers between devices  45 us (13%)
  starting transfers between devices  36.4 us (11%)
  local copies, waits for them, and re-layouts  6.28 us (2%)
    pallas_call x3, Pallas kernels, attend(): pl.pallas_call(functools.partial(attend_kernel, n_seg=n, coords=coords, s...  214 us
    pallas_call x4, Pallas kernels, project(): pl.pallas_call(project_kernel, grid=(steps,), in_specs=specs + [pl.BlockS...  17.9 us
    ppermute x2, waiting for transfers between devices, shards(): over = lax.ppermute(picked, 'ha', chips)  14.9 us
    ppermute x2, waiting for transfers between devices, shards(): corner = lax.ppermute(over, ('ha', 'wa'), turn)  14.7 us
    ppermute x4, starting transfers between devices, spread(): lax.ppermute(piece, 'hd', hd_pairs(-1))  10.4 us
    ppermute x4, waiting for transfers between devices, spread(): lax.ppermute(piece, 'hd', hd_pairs(-1))  8.3 us
  transfers between devices with their start and end apart: 37, of which 8 were waited for; matrix products, arithmetic and copies ran while one was open for 0% of the time, Pallas kernels for 72%

profile of v2, /device:TPU:48, one launch (start us, length us, event | category | flops | bytes accessed | tf_op | source)
XLA Modules:
  0.0 333.7 jit_solution(2241127338009988902)
XLA Ops:
  0.0 2.8 pack.3
  3.3 2.2 pack.2
  7.8 2.0 choose.3
  13.7 1.8 choose.2
  15.5 2.0 collective-permute-start.2
  17.4 3.7 %collective-permute-done.4.refs_6_ = bf16[1,2,768,128]{3,2,1,0:T(8,128)(2,1)S(1)} collective-permute-done((bf16[1,2,768,128]{3,2,1,0:T(8,128)(2,1)S(1)}, bf16[1,2,768,128]{3,2,1,0:T(8,128)(2,1)S(1)}, u32[]{:S(2)}, u32[]{:S(2)}) %collective-permute-start.4) | collective-permute-done | bytes 393248 | tf_op jit(solution)/shard_map/ppermute | solution.py:303
  23.3 14.9 %collective-permute-done.2.refs_4_ = bf16[1,2,768,128]{3,2,1,0:T(8,128)(2,1)S(1)} collective-permute-done((bf16[1,2,768,128]{3,2,1,0:T(8,128)(2,1)}, bf16[1,2,768,128]{3,2,1,0:T(8,128)(2,1)S(1)}, u32[]{:S(2)}, u32[]{:S(2)}) %collective-permute-start.2) | collective-permute-done | bytes 393248 | tf_op jit(solution)/shard_map/ppermute | solution.py:307
  40.2 14.7 %collective-permute-done.8.refs_10_ = bf16[1,2,768,128]{3,2,1,0:T(8,128)(2,1)} collective-permute-done((bf16[1,2,768,128]{3,2,1,0:T(8,128)(2,1)S(1)}, bf16[1,2,768,128]{3,2,1,0:T(8,128)(2,1)}, u32[]{:S(2)}, u32[]{:S(2)}) %collective-permute-start.8) | collective-permute-done | bytes 393248 | tf_op jit(solution)/shard_map/ppermute | solution.py:308
  57.4 3.3 cut.1
  62.3 71.4 %attend.3.refs_0_ = bf16[12,8,16,128]{3,2,1,0:T(8,128)(2,1)} custom-call(s32[3,2,1,2]{3,2,1,0:T(1,128)} %copy.8.rad, bf16[12,8,16,384]{3,2,1,0:T(8,128)(2,1)} %q.5, bf16[256,384]{1,0:T(8,128)(2,1)} %tk.5, bf16[256,384]{1,0:T(8,128)(2,1)} %tv.5, bf16[1,2,768,128]{3,2,1,0:T(8,128)(2,1)} %bitcast.16, bf16[1,2,768,128]{3,2,1,0:T(8,128)(2,1)} %bitcast.20, ...), custom_call_target="tpu_custom_call" | custom-call | flops 6000000000 | bytes 6000000 | tf_op jit(solution)/shard_map/attend/pallas_call | solution.py:146
  133.7 1.8 collective-permute-start.30
  135.6 1.9 collective-permute-start.31
  138.0 2.6 collective-permute-start.23
  140.7 71.4 %attend.4.refs_1_ = bf16[12,8,16,128]{3,2,1,0:T(8,128)(2,1)} custom-call(s32[3,2,1,2]{3,2,1,0:T(1,128)} %copy.8.rad, bf16[12,8,16,384]{3,2,1,0:T(8,128)(2,1)} %q.5, bf16[256,384]{1,0:T(8,128)(2,1)} %tk.5, bf16[256,384]{1,0:T(8,128)(2,1)} %tv.5, bf16[2,2,768,128]{3,2,1,0:T(8,128)(2,1)} %bitcast.6, bf16[2,2,768,128]{3,2,1,0:T(8,128)(2,1)} %bitcast.11, ...), custom_call_target="tpu_custom_call" | custom-call | flops 6000000000 | bytes 6000000 | tf_op jit(solution)/shard_map/attend/pallas_call | solution.py:146
  212.8 71.4 %attend.5 = (bf16[6,8,16,128]{3,2,1,0:T(8,128)(2,1)}, bf16[6,8,16,128]{3,2,1,0:T(8,128)(2,1)}) custom-call(s32[3,2,1,2]{3,2,1,0:T(1,128)} %copy.8.rad, bf16[12,8,16,384]{3,2,1,0:T(8,128)(2,1)} %q.5, bf16[256,384]{1,0:T(8,128)(2,1)} %tk.5, bf16[256,384]{1,0:T(8,128)(2,1)} %tv.5, bf16[2,2,768,128]{3,2,1,0:T(8,128)(2,1)} %bitcast.7, ...), custom_call_target="tpu_custom_call" | custom-call | flops 6000000000 | bytes 6000000 | tf_op jit(solution)/shard_map/attend/pallas_call | solution.py:146
  284.8 2.5 collective-permute-start.21
  289.5 2.5 collective-permute-start.34
  293.2 8.3 %collective-permute-done.34.refs_8_ = bf16[6,8,16,128]{3,2,1,0:T(8,128)(2,1)S(1)} collective-permute-done((bf16[6,8,16,128]{3,2,1,0:T(8,128)(2,1)}, bf16[6,8,16,128]{3,2,1,0:T(8,128)(2,1)S(1)}, u32[]{:S(2)}, u32[]{:S(2)}) %collective-permute-start.34) | collective-permute-done | bytes 196640 | tf_op jit(solution)/shard_map/ppermute | solution.py:324
  301.8 4.4 %collective-permute-start.25 = (bf16[6,8,16,128]{3,2,1,0:T(8,128)(2,1)}, bf16[6,8,16,128]{3,2,1,0:T(8,128)(2,1)S(1)}, u32[]{:S(2)}, u32[]{:S(2)}) collective-permute-start(bf16[6,8,16,128]{3,2,1,0:T(8,128)(2,1)} %get-tuple-element.19.refs_2_), channel_id=1, source_target_pairs={{0,3},{1,0},{2,1},{3,2},{4,7},{5,4},{6,5},{7,6},{8,11},{9,8},{10,9... | collective-permute-start | bytes 589832 | tf_op jit(solution)/shard_map/ppermute | solution.py:324
  308.3 4.4 %project.7 = bf16[6,8,16,384]{3,2,1,0:T(8,128)(2,1)} custom-call(bf16[12,8,16,128]{3,2,1,0:T(8,128)(2,1)} %attend.3.refs_0_, bf16[12,8,16,128]{3,2,1,0:T(8,128)(2,1)} %attend.4.refs_1_, bf16[6,8,16,128]{3,2,1,0:T(8,128)(2,1)} %get-tuple-element.24.refs_2_, bf16[12,8,16,128]{3,2,1,0:T(8,128)(2,1)} %copy-done.4, bf16[12,8,16,128]{3,2,1,0:T(8,128)(2,1)} %copy-done.7, ...), custom_call_target="tpu_custom_call" | custom-call | flops 1000000000 | bytes 4500000 | tf_op jit(solution)/shard_map/project/pallas_call | solution.py:261
  312.7 3.0 collective-permute-start.36
  316.5 4.3 %project.5 = bf16[6,8,16,384]{3,2,1,0:T(8,128)(2,1)} custom-call(bf16[12,8,16,128]{3,2,1,0:T(8,128)(2,1)} %attend.3.refs_0_, bf16[12,8,16,128]{3,2,1,0:T(8,128)(2,1)} %attend.4.refs_1_, bf16[6,8,16,128]{3,2,1,0:T(8,128)(2,1)} %get-tuple-element.19.refs_2_, bf16[12,8,16,128]{3,2,1,0:T(8,128)(2,1)} %copy-done.4, bf16[12,8,16,128]{3,2,1,0:T(8,128)(2,1)} %copy-done.7, ...), custom_call_target="tpu_custom_call" | custom-call | flops 1000000000 | bytes 4500000 | tf_op jit(solution)/shard_map/project/pallas_call | solution.py:261
  321.3 4.6 %project.6 = f32[6,8,16,384]{3,2,1,0:T(8,128)} custom-call(bf16[12,8,16,128]{3,2,1,0:T(8,128)(2,1)} %attend.3.refs_0_, bf16[12,8,16,128]{3,2,1,0:T(8,128)(2,1)} %attend.4.refs_1_, bf16[6,8,16,128]{3,2,1,0:T(8,128)(2,1)} %get-tuple-element.24.refs_2_, bf16[12,8,16,128]{3,2,1,0:T(8,128)(2,1)} %copy-done.4, bf16[12,8,16,128]{3,2,1,0:T(8,128)(2,1)} %copy-done.7, ...), custom_call_target="tpu_custom_call" | custom-call | flops 1000000000 | bytes 4500000 | tf_op jit(solution)/shard_map/project/pallas_call | solution.py:261
  325.9 4.7 %project.4 = f32[6,8,16,384]{3,2,1,0:T(8,128)} custom-call(bf16[12,8,16,128]{3,2,1,0:T(8,128)(2,1)} %attend.3.refs_0_, bf16[12,8,16,128]{3,2,1,0:T(8,128)(2,1)} %attend.4.refs_1_, bf16[6,8,16,128]{3,2,1,0:T(8,128)(2,1)} %get-tuple-element.19.refs_2_, bf16[12,8,16,128]{3,2,1,0:T(8,128)(2,1)} %copy-done.4, bf16[12,8,16,128]{3,2,1,0:T(8,128)(2,1)} %copy-done.7, ...), custom_call_target="tpu_custom_call" | custom-call | flops 1000000000 | bytes 4500000 | tf_op jit(solution)/shard_map/project/pallas_call | solution.py:261
  (132 shorter events, 26.7 us)
Async XLA Ops:
  9.9 28.3 %collective-permute-start.12 = (bf16[2,2,768,128]{3,2,1,0:T(8,128)(2,1)}, bf16[2,2,768,128]{3,2,1,0:T(8,128)(2,1)}, u32[]{:S(2)}, u32[]{:S(2)}) collective-permute-start(bf16[2,2,768,128]{3,2,1,0:T(8,128)(2,1)} %choose.3), channel_id=1, source_target_pairs={{0,64},{32,96},{64,0},{96,32},{1,65},{33,97},{65,1},{97,33},{2,66}... | collective-permute-start | bytes 2359304 | tf_op jit(solution)/shard_map/ppermute | solution.py:307
  15.5 22.7 %collective-permute-start.2 = (bf16[1,2,768,128]{3,2,1,0:T(8,128)(2,1)}, bf16[1,2,768,128]{3,2,1,0:T(8,128)(2,1)S(1)}, u32[]{:S(2)}, u32[]{:S(2)}) collective-permute-start(bf16[1,2,768,128]{3,2,1,0:T(8,128)(2,1)} %choose.2), channel_id=1, source_target_pairs={{0,64},{32,96},{64,0},{96,32},{1,65},{33,97},{65,1},{97,33},{2,66}... | collective-permute-start | bytes 1179656 | tf_op jit(solution)/shard_map/ppermute | solution.py:307
  21.2 17.5 %collective-permute-start.6 = (bf16[1,2,768,128]{3,2,1,0:T(8,128)(2,1)S(1)}, bf16[1,2,768,128]{3,2,1,0:T(8,128)(2,1)S(1)}, u32[]{:S(2)}, u32[]{:S(2)}) collective-permute-start(bf16[1,2,768,128]{3,2,1,0:T(8,128)(2,1)S(1)} %collective-permute-done.4.refs_6_), channel_id=1, source_target_pairs={{0,32},{32,0},{64,96},{96,64},{1,33},{33,1},{65,97},{97,65},{2,34}... | collective-permute-start | bytes 1179656 | tf_op jit(solution)/shard_map/ppermute | solution.py:298
  21.2 33.7 %collective-permute-start.14 = (bf16[2,2,768,128]{3,2,1,0:T(8,128)(2,1)S(1)}, bf16[2,2,768,128]{3,2,1,0:T(8,128)(2,1)}, u32[]{:S(2)}, u32[]{:S(2)}) collective-permute-start(bf16[2,2,768,128]{3,2,1,0:T(8,128)(2,1)S(1)} %bitcast.13), channel_id=1, source_target_pairs={{0,8},{8,16},{16,24},{24,0},{1,9},{9,17},{17,25},{25,1},{2,10},{10... | collective-permute-start | bytes 2359304 | tf_op jit(solution)/shard_map/ppermute | solution.py:303
  22.5 32.9 %collective-permute-start.15 = (bf16[2,2,768,128]{3,2,1,0:T(8,128)(2,1)S(1)}, bf16[2,2,768,128]{3,2,1,0:T(8,128)(2,1)S(1)}, u32[]{:S(2)}, u32[]{:S(2)}) collective-permute-start(bf16[2,2,768,128]{3,2,1,0:T(8,128)(2,1)S(1)} %bitcast.8), channel_id=1, source_target_pairs={{8,0},{16,8},{24,16},{0,24},{9,1},{17,9},{25,17},{1,25},{10,2},{18... | collective-permute-start | bytes 2359304 | tf_op jit(solution)/shard_map/ppermute | solution.py:304
  38.2 18.2 %collective-permute-start.18 = (bf16[2,2,768,128]{3,2,1,0:T(8,128)(2,1)}, bf16[2,2,768,128]{3,2,1,0:T(8,128)(2,1)}, u32[]{:S(2)}, u32[]{:S(2)}) collective-permute-start(bf16[2,2,768,128]{3,2,1,0:T(8,128)(2,1)} %collective-permute-done.12.refs_4_), channel_id=1, source_target_pairs={{8,0},{16,8},{24,16},{0,24},{32,40},{40,48},{48,56},{56,32},{72,64... | collective-permute-start | bytes 2359304 | tf_op jit(solution)/shard_map/ppermute | solution.py:308
  38.7 16.2 %collective-permute-start.8 = (bf16[1,2,768,128]{3,2,1,0:T(8,128)(2,1)S(1)}, bf16[1,2,768,128]{3,2,1,0:T(8,128)(2,1)}, u32[]{:S(2)}, u32[]{:S(2)}) collective-permute-start(bf16[1,2,768,128]{3,2,1,0:T(8,128)(2,1)S(1)} %collective-permute-done.2.refs_4_), channel_id=1, source_target_pairs={{8,0},{16,8},{24,16},{0,24},{32,40},{40,48},{48,56},{56,32},{72,64... | collective-permute-start | bytes 1179656 | tf_op jit(solution)/shard_map/ppermute | solution.py:308
  40.1 15.4 %collective-permute-start.3 = (bf16[1,2,768,128]{3,2,1,0:T(8,128)(2,1)S(1)}, bf16[1,2,768,128]{3,2,1,0:T(8,128)(2,1)S(1)}, u32[]{:S(2)}, u32[]{:S(2)}) collective-permute-start(bf16[1,2,768,128]{3,2,1,0:T(8,128)(2,1)S(1)} %collective-permute-done.2.refs_4_), channel_id=1, source_target_pairs={{0,32},{32,0},{64,96},{96,64},{1,33},{33,1},{65,97},{97,65},{2,34}... | collective-permute-start | bytes 1179656 | tf_op jit(solution)/shard_map/ppermute | solution.py:298
  54.9 78.8 %collective-permute-start.16 = (bf16[2,2,768,128]{3,2,1,0:T(8,128)(2,1)}, bf16[2,2,768,128]{3,2,1,0:T(8,128)(2,1)S(1)}, u32[]{:S(2)}, u32[]{:S(2)}) collective-permute-start(bf16[2,2,768,128]{3,2,1,0:T(8,128)(2,1)} %collective-permute-done.14.refs_6_), channel_id=1, source_target_pairs={{0,32},{32,0},{64,96},{96,64},{1,33},{33,1},{65,97},{97,65},{2,34}... | collective-permute-start | bytes 2359304 | tf_op jit(solution)/shard_map/ppermute | solution.py:298
  55.4 80.1 %collective-permute-start.17 = (bf16[2,2,768,128]{3,2,1,0:T(8,128)(2,1)S(1)}, bf16[2,2,768,128]{3,2,1,0:T(8,128)(2,1)}, u32[]{:S(2)}, u32[]{:S(2)}) collective-permute-start(bf16[2,2,768,128]{3,2,1,0:T(8,128)(2,1)S(1)} %collective-permute-done.15.refs_7_), channel_id=1, source_target_pairs={{0,32},{32,0},{64,96},{96,64},{1,33},{33,1},{65,97},{97,65},{2,34}... | collective-permute-start | bytes 2359304 | tf_op jit(solution)/shard_map/ppermute | solution.py:298
  55.5 81.9 %collective-permute-start.13 = (bf16[2,2,768,128]{3,2,1,0:T(8,128)(2,1)}, bf16[2,2,768,128]{3,2,1,0:T(8,128)(2,1)}, u32[]{:S(2)}, u32[]{:S(2)}) collective-permute-start(bf16[2,2,768,128]{3,2,1,0:T(8,128)(2,1)} %collective-permute-done.12.refs_4_), channel_id=1, source_target_pairs={{0,32},{32,0},{64,96},{96,64},{1,33},{33,1},{65,97},{97,65},{2,34}... | collective-permute-start | bytes 2359304 | tf_op jit(solution)/shard_map/ppermute | solution.py:298
  56.4 81.7 %collective-permute-start.19 = (bf16[2,2,768,128]{3,2,1,0:T(8,128)(2,1)}, bf16[2,2,768,128]{3,2,1,0:T(8,128)(2,1)}, u32[]{:S(2)}, u32[]{:S(2)}) collective-permute-start(bf16[2,2,768,128]{3,2,1,0:T(8,128)(2,1)} %collective-permute-done.18.refs_10_), channel_id=1, source_target_pairs={{0,32},{32,0},{64,96},{96,64},{1,33},{33,1},{65,97},{97,65},{2,34}... | collective-permute-start | bytes 2359304 | tf_op jit(solution)/shard_map/ppermute | solution.py:298
  60.7 151.4 %collective-permute-start.29 = (bf16[2,384,384]{2,1,0:T(8,128)(2,1)}, bf16[2,384,384]{2,1,0:T(8,128)(2,1)S(1)}, u32[]{:S(2)}, u32[]{:S(2)}) collective-permute-start(bf16[2,384,384]{2,1,0:T(8,128)(2,1)} %get-tuple-element.21), channel_id=1, source_target_pairs={{0,1},{1,2},{2,3},{3,0},{4,5},{5,6},{6,7},{7,4},{8,9},{9,10},{10,1... | collective-permute-start | bytes 1769480 | tf_op jit(solution)/shard_map/ppermute | solution.py:316
  133.7 150.4 %collective-permute-start.30 = (bf16[2,384,384]{2,1,0:T(8,128)(2,1)}, bf16[2,384,384]{2,1,0:T(8,128)(2,1)S(1)}, u32[]{:S(2)}, u32[]{:S(2)}) collective-permute-start(bf16[2,384,384]{2,1,0:T(8,128)(2,1)} %get-tuple-element.22), channel_id=1, source_target_pairs={{0,3},{1,0},{2,1},{3,2},{4,7},{5,4},{6,5},{7,6},{8,11},{9,8},{10,9... | collective-permute-start | bytes 1769480 | tf_op jit(solution)/shard_map/ppermute | solution.py:317
  135.6 149.3 %collective-permute-start.31 = (bf16[2,384,384]{2,1,0:T(8,128)(2,1)}, bf16[2,384,384]{2,1,0:T(8,128)(2,1)S(1)}, u32[]{:S(2)}, u32[]{:S(2)}) collective-permute-start(bf16[2,384,384]{2,1,0:T(8,128)(2,1)} %get-tuple-element.23), channel_id=1, source_target_pairs={{0,2},{1,3},{2,0},{3,1},{4,6},{5,7},{6,4},{7,5},{8,10},{9,11},{10,... | collective-permute-start | bytes 1769480 | tf_op jit(solution)/shard_map/ppermute | solution.py:318
  137.4 149.9 %collective-permute-start.20 = (bf16[12,8,16,128]{3,2,1,0:T(8,128)(2,1)}, bf16[12,8,16,128]{3,2,1,0:T(8,128)(2,1)S(1)}, u32[]{:S(2)}, u32[]{:S(2)}) collective-permute-start(bf16[12,8,16,128]{3,2,1,0:T(8,128)(2,1)} %attend.3.refs_0_), channel_id=1, source_target_pairs={{0,1},{1,2},{2,3},{3,0},{4,5},{5,6},{6,7},{7,4},{8,9},{9,10},{10,1... | collective-permute-start | bytes 1179656 | tf_op jit(solution)/shard_map/ppermute | solution.py:323
  138.0 150.1 %collective-permute-start.23 = (bf16[12,8,16,128]{3,2,1,0:T(8,128)(2,1)}, bf16[12,8,16,128]{3,2,1,0:T(8,128)(2,1)S(1)}, u32[]{:S(2)}, u32[]{:S(2)}) collective-permute-start(bf16[12,8,16,128]{3,2,1,0:T(8,128)(2,1)} %attend.3.refs_0_), channel_id=1, source_target_pairs={{0,3},{1,0},{2,1},{3,2},{4,7},{5,4},{6,5},{7,6},{8,11},{9,8},{10,9... | collective-permute-start | bytes 1179656 | tf_op jit(solution)/shard_map/ppermute | solution.py:324
  212.2 77.3 %collective-permute-start.26 = (bf16[12,8,16,128]{3,2,1,0:T(8,128)(2,1)S(1)}, bf16[12,8,16,128]{3,2,1,0:T(8,128)(2,1)}, u32[]{:S(2)}, u32[]{:S(2)}) collective-permute-start(bf16[12,8,16,128]{3,2,1,0:T(8,128)(2,1)S(1)} %copy-done.3), channel_id=1, source_target_pairs={{0,2},{1,3},{2,0},{3,1},{4,6},{5,7},{6,4},{7,5},{8,10},{9,11},{10,... | collective-permute-start | bytes 1179656 | tf_op jit(solution)/shard_map/ppermute | solution.py:325
  284.8 21.4 %collective-permute-start.21 = (bf16[12,8,16,128]{3,2,1,0:T(8,128)(2,1)S(1)}, bf16[12,8,16,128]{3,2,1,0:T(8,128)(2,1)S(1)}, u32[]{:S(2)}, u32[]{:S(2)}) collective-permute-start(bf16[12,8,16,128]{3,2,1,0:T(8,128)(2,1)S(1)} %copy-done.6), channel_id=1, source_target_pairs={{0,1},{1,2},{2,3},{3,0},{4,5},{5,6},{6,7},{7,4},{8,9},{9,10},{10,1... | collective-permute-start | bytes 1179656 | tf_op jit(solution)/shard_map/ppermute | solution.py:323
  287.3 19.4 %collective-permute-start.24 = (bf16[12,8,16,128]{3,2,1,0:T(8,128)(2,1)S(1)}, bf16[12,8,16,128]{3,2,1,0:T(8,128)(2,1)S(1)}, u32[]{:S(2)}, u32[]{:S(2)}) collective-permute-start(bf16[12,8,16,128]{3,2,1,0:T(8,128)(2,1)S(1)} %copy-done.6), channel_id=1, source_target_pairs={{0,3},{1,0},{2,1},{3,2},{4,7},{5,4},{6,5},{7,6},{8,11},{9,8},{10,9... | collective-permute-start | bytes 1179656 | tf_op jit(solution)/shard_map/ppermute | solution.py:324
  288.1 18.6 %collective-permute-start.27 = (bf16[12,8,16,128]{3,2,1,0:T(8,128)(2,1)S(1)}, bf16[12,8,16,128]{3,2,1,0:T(8,128)(2,1)S(1)}, u32[]{:S(2)}, u32[]{:S(2)}) collective-permute-start(bf16[12,8,16,128]{3,2,1,0:T(8,128)(2,1)S(1)} %copy-done.6), channel_id=1, source_target_pairs={{0,2},{1,3},{2,0},{3,1},{4,6},{5,7},{6,4},{7,5},{8,10},{9,11},{10,... | collective-permute-start | bytes 1179656 | tf_op jit(solution)/shard_map/ppermute | solution.py:325
  301.5 14.2 %collective-permute-start.22 = (bf16[6,8,16,128]{3,2,1,0:T(8,128)(2,1)}, bf16[6,8,16,128]{3,2,1,0:T(8,128)(2,1)S(1)}, u32[]{:S(2)}, u32[]{:S(2)}) collective-permute-start(bf16[6,8,16,128]{3,2,1,0:T(8,128)(2,1)} %get-tuple-element.19.refs_2_), channel_id=1, source_target_pairs={{0,1},{1,2},{2,3},{3,0},{4,5},{5,6},{6,7},{7,4},{8,9},{9,10},{10,1... | collective-permute-start | bytes 589832 | tf_op jit(solution)/shard_map/ppermute | solution.py:323
  301.8 13.9 %collective-permute-start.25 = (bf16[6,8,16,128]{3,2,1,0:T(8,128)(2,1)}, bf16[6,8,16,128]{3,2,1,0:T(8,128)(2,1)S(1)}, u32[]{:S(2)}, u32[]{:S(2)}) collective-permute-start(bf16[6,8,16,128]{3,2,1,0:T(8,128)(2,1)} %get-tuple-element.19.refs_2_), channel_id=1, source_target_pairs={{0,3},{1,0},{2,1},{3,2},{4,7},{5,4},{6,5},{7,6},{8,11},{9,8},{10,9... | collective-permute-start | bytes 589832 | tf_op jit(solution)/shard_map/ppermute | solution.py:324
  312.7 17.9 %collective-permute-start.36 = (bf16[6,8,16,384]{3,2,1,0:T(8,128)(2,1)}, bf16[6,8,16,384]{3,2,1,0:T(8,128)(2,1)S(1)}, u32[]{:S(2)}, u32[]{:S(2)}) collective-permute-start(bf16[6,8,16,384]{3,2,1,0:T(8,128)(2,1)} %project.7), channel_id=1, source_target_pairs={{0,4},{1,5},{2,6},{3,7},{4,0},{5,1},{6,2},{7,3},{8,12},{9,13},{10,... | collective-permute-start | bytes 1769480 | tf_op jit(solution)/shard_map/ppermute | solution.py:341
  (46 other events, 642.4 us)

commit v3 on v2

--- a/solution.py
+++ b/solution.py
@@ -11,7 +11,7 @@
 NT=(((1,),(1,)),((),()))
 
 
-def attend_kernel(rad, q, tk, tv, *refs, n_seg, coords, sub, times, split, QB, KW):
+def attend_kernel(rad, q, tk, tv, *refs, n_seg, coords, subs, times, split, QB, KW):
     segs = refs[:n_seg]
     qs, kbuf, vbuf, tvb, mref, peak, acc, lst, cnt, sems = refs[-10:]
     out = refs[n_seg:-10]
@@ -20,8 +20,8 @@
     ha, wa, n_ha, n_wa = coords()
     copies=[]
     for i,s in enumerate(segs):
-        copies.append(pltpu.make_async_copy(s.at[sub,0], kbuf.at[i], sems.at[2*i]))
-        copies.append(pltpu.make_async_copy(s.at[sub,1], vbuf.at[i,:,pl.ds(0,128)], sems.at[2*i+1]))
+        copies.append(pltpu.make_async_copy(s.at[subs[i],0], kbuf.at[i], sems.at[2*i]))
+        copies.append(pltpu.make_async_copy(s.at[subs[i],1], vbuf.at[i,:,pl.ds(0,128)], sems.at[2*i+1]))
     for c in copies: c.start()
     is_odd = ha % 2
     across_ok = jnp.where(is_odd==1, ha + 1 < n_ha, ha > 0).astype(jnp.int32)
@@ -139,12 +139,12 @@
         ref[f:f+6,:,8*e:8*e+8,:]=(acc[qt,:,0:128]/acc[qt,:,128:256]).astype(jnp.bfloat16).reshape(6,8,8,HEAD)
 
 
-def attend(rad,q,tk,tv,segs,h,sub,coords,times=(0,1),split=True,QB=192,KW=768):
+def attend(rad,q,tk,tv,segs,h,subs,coords,times=(0,1),split=True,QB=192,KW=768):
     n=len(segs); nt=2*len(times); frames=6*len(times)
     first=times[0] if len(times)==1 else 0
     size=6 if split else frames
     return pl.pallas_call(
-        functools.partial(attend_kernel,n_seg=n,coords=coords,sub=sub,times=times,split=split,QB=QB,KW=KW),
+        functools.partial(attend_kernel,n_seg=n,coords=coords,subs=subs,times=times,split=split,QB=QB,KW=KW),
         grid=(1,),
         in_specs=[pl.BlockSpec(memory_space=pltpu.SMEM),
             pl.BlockSpec((frames,8,16,HEAD),lambda i:(first,0,0,h)),
@@ -166,11 +166,11 @@
 
 
 def pack_kernel(*refs):
-    low, high = refs[-2:]
-    for i in range(low.shape[0]):
-        for col, ref in enumerate((low, high)):
+    count = len(refs) // 4
+    for i in range(count):
+        for col in range(2):
             for j in range(2):
-                ref[i, j] = refs[2 * i + j][:, :, 8 * col : 8 * col + 8, :]
+                refs[2 * count + 2 * i + col][0, j] = refs[2 * i + j][:, :, 8 * col : 8 * col + 8, :]
 
 
 def pack(keys, values, first, count):
@@ -179,39 +179,46 @@
         for h in range(first, first + count)
         for _ in range(2)
     ]
-    shape = (count, 2, 12, 8, 8, HEAD)
+    shape = (1, 2, 12, 8, 8, HEAD)
     outs = pl.pallas_call(
         pack_kernel,
         grid=(1,),
         in_specs=specs,
-        out_specs=[pl.BlockSpec(shape, lambda i: (0,) * 6)] * 2,
-        out_shape=[jax.ShapeDtypeStruct(shape, jnp.bfloat16)] * 2,
+        out_specs=[pl.BlockSpec(shape, lambda i: (0,) * 6)] * (2 * count),
+        out_shape=[jax.ShapeDtypeStruct(shape, jnp.bfloat16)] * (2 * count),
         cost_estimate=pl.CostEstimate(flops=500_000_000, transcendentals=0, bytes_accessed=1_600_000),
         name="pack",
     )(*[keys, values] * count)
-    return [out.reshape(count, 2, 768, HEAD) for out in outs]
-
-
-def choose_kernel(own_low, own_high, partner_low, partner_high, out, sem):
+    return [out.reshape(1, 2, 768, HEAD) for out in outs]
+
+
+def choose_kernel(*refs):
+    count = (len(refs) - 2) // 4
+    out, sem = refs[-2:]
     ha = lax.axis_index("ha")
     inner = (ha > 0) & (ha + 1 < lax.axis_size("ha"))
     odd = ha % 2 == 1
-    for is_inner, refs in ((True, (own_low, own_high)), (False, (partner_low, partner_high))):
-        for is_odd, ref in enumerate(refs):
-
-            @pl.when((inner == is_inner) & (odd == bool(is_odd)))
-            def _():
-                copy = pltpu.make_async_copy(ref, out, sem)
+    for source in range(4):
+
+        @pl.when((inner == (source < 2)) & (odd == (source % 2 == 1)))
+        def _():
+            copies = [
+                pltpu.make_async_copy(refs[4 * i + source].at[0], out.at[i], sem.at[i])
+                for i in range(count)
+            ]
+            for copy in copies:
                 copy.start()
+            for copy in copies:
                 copy.wait()
 
 
 def choose(*pieces):
+    count = len(pieces) // 4
     return pl.pallas_call(
         choose_kernel,
-        in_specs=[pl.BlockSpec(memory_space=pltpu.HBM)] * 4,
-        out_shape=jax.ShapeDtypeStruct(pieces[0].shape, jnp.bfloat16),
-        scratch_shapes=[pltpu.SemaphoreType.DMA],
+        in_specs=[pl.BlockSpec(memory_space=pltpu.HBM)] * len(pieces),
+        out_shape=jax.ShapeDtypeStruct((count, *pieces[0].shape[1:]), jnp.bfloat16),
+        scratch_shapes=[pltpu.SemaphoreType.DMA((count,))],
         cost_estimate=pl.CostEstimate(flops=200_000_000, transcendentals=0, bytes_accessed=800_000),
         name="choose",
     )(*pieces)
@@ -299,17 +306,24 @@
 
     windows = []
     for first, count in GROUPS:
-        low, high = pack(video_keys, video_values, first, count)
-        from_left = lax.ppermute(high, "wa", ring)
-        from_right = lax.ppermute(low, "wa", back)
-        partner_low, partner_high = swap(low), swap(high)
-        picked = choose(low, high, partner_low, partner_high)
+        own = pack(video_keys, video_values, first, count)
+        near, picks = [], []
+        for i in range(count):
+            low, high = own[2 * i : 2 * i + 2]
+            from_left = lax.ppermute(high, "wa", ring)
+            from_right = lax.ppermute(low, "wa", back)
+            partner_low, partner_high = swap(low), swap(high)
+            picks += [low, high, partner_low, partner_high]
+            near.append((low, high, partner_low, partner_high, from_left, from_right,
+                         swap(from_left), swap(from_right)))
+        picked = choose(*picks)
         over = lax.ppermute(picked, "ha", chips)
         corner = lax.ppermute(over, ("ha", "wa"), turn)
-        window = (low, high, partner_low, partner_high, over, swap(over),
-                  from_left, from_right, swap(from_left), swap(from_right),
-                  corner, swap(corner))
-        windows += [(window, i) for i in range(count)]
+        far = (over, swap(over)), (corner, swap(corner))
+        for i in range(count):
+            windows.append(
+                ((*near[i][:4], *far[0], *near[i][4:], *far[1]), (0,) * 4 + (i,) * 2 + (0,) * 4 + (i,) * 2)
+            )
     pieces = cut(out_weight)
     weights = [
         pieces[0],
@@ -326,8 +340,8 @@
         ]
 
     def head(h, times, split):
-        window, sub = windows[h]
-        return attend(tile_radius, queries, text_keys, text_values, window, h, sub, place, times, split)
+        window, subs = windows[h]
+        return attend(tile_radius, queries, text_keys, text_values, window, h, subs, place, times, split)
 
     (first_head,) = head(0, (0, 1), False)
     (second_head,) = head(1, (0, 1), False)

time: 334 us -> 342 us (1.024)
  waiting for transfers between devices: 45 us -> 49.7 us
  starting transfers between devices: 36.4 us -> 40.3 us
    ppermute x2 -> x3, waiting for transfers between devices: 0.01 us -> 16.3 us  [shards(): from_right = lax.ppermute(low, 'wa', back)]
    ppermute x2, waiting for transfers between devices: 14.7 us -> 4.32 us  [shards(): corner = lax.ppermute(over, ('ha', 'wa'), turn)]
    ppermute x2, waiting for transfers between devices: 14.9 us -> 8.01 us  [shards(): over = lax.ppermute(picked, 'ha', chips)]
    ppermute x2 -> x3, waiting for transfers between devices: 3.73 us -> 9.04 us  [shards(): from_left = lax.ppermute(high, 'wa', ring)]
  transfers between devices with their start and end apart: 37 -> 43, of which waited for: 8 -> 15; matrix products, arithmetic and copies ran while one was open for 0% -> 0% of each run, Pallas kernels for 72% -> 70%
where the time goes in v3:
time: 342 us
  Pallas kernels  245 us (72%)
  waiting for transfers between devices  49.7 us (15%)
  starting transfers between devices  40.3 us (12%)
  local copies, waits for them, and re-layouts  5.49 us (2%)
    pallas_call x3, Pallas kernels, attend(): pl.pallas_call(functools.partial(attend_kernel, n_seg=n, coords=coords, s...  214 us
    pallas_call x4, Pallas kernels, project(): pl.pallas_call(project_kernel, grid=(steps,), in_specs=specs + [pl.BlockS...  17.9 us
    ppermute x3, waiting for transfers between devices, shards(): from_right = lax.ppermute(low, 'wa', back)  16.3 us
    ppermute x4, starting transfers between devices, spread(): lax.ppermute(piece, 'hd', hd_pairs(-1))  10.4 us
    ppermute x3, waiting for transfers between devices, shards(): from_left = lax.ppermute(high, 'wa', ring)  9.04 us
    ppermute x4, waiting for transfers between devices, spread(): lax.ppermute(piece, 'hd', hd_pairs(-1))  8.45 us
    ppermute x2, waiting for transfers between devices, shards(): over = lax.ppermute(picked, 'ha', chips)  8.01 us
  transfers between devices with their start and end apart: 43, of which 15 were waited for; matrix products, arithmetic and copies ran while one was open for 0% of the time, Pallas kernels for 70%

profile of v3, /device:TPU:48, one launch (start us, length us, event | category | flops | bytes accessed | tf_op | source)
XLA Modules:
  0.0 341.8 jit_solution(11379770328159297437)
XLA Ops:
  0.0 2.9 pack.3
  7.5 2.0 choose.3
  9.7 2.2 pack.2
  20.3 4.3 %collective-permute-done.22.refs_6_ = bf16[1,2,768,128]{3,2,1,0:T(8,128)(2,1)} collective-permute-done((bf16[1,2,768,128]{3,2,1,0:T(8,128)(2,1)S(1)}, bf16[1,2,768,128]{3,2,1,0:T(8,128)(2,1)}, u32[]{:S(2)}, u32[]{:S(2)}) %collective-permute-start.22) | collective-permute-done | bytes 393248 | tf_op jit(solution)/shard_map/ppermute | solution.py:313
  25.9 4.4 %collective-permute-done.14.refs_4_ = bf16[2,2,768,128]{3,2,1,0:T(8,128)(2,1)} collective-permute-done((bf16[2,2,768,128]{3,2,1,0:T(8,128)(2,1)}, bf16[2,2,768,128]{3,2,1,0:T(8,128)(2,1)}, u32[]{:S(2)}, u32[]{:S(2)}) %collective-permute-start.14) | collective-permute-done | bytes 786464 | tf_op jit(solution)/shard_map/ppermute | solution.py:320
  34.3 3.6 %collective-permute-done.2.refs_4_ = bf16[1,2,768,128]{3,2,1,0:T(8,128)(2,1)} collective-permute-done((bf16[1,2,768,128]{3,2,1,0:T(8,128)(2,1)}, bf16[1,2,768,128]{3,2,1,0:T(8,128)(2,1)}, u32[]{:S(2)}, u32[]{:S(2)}) %collective-permute-start.2) | collective-permute-done | bytes 393248 | tf_op jit(solution)/shard_map/ppermute | solution.py:320
  38.4 3.0 collective-permute-done.4.refs_6_
  41.4 12.1 %collective-permute-done.5.refs_7_ = bf16[1,2,768,128]{3,2,1,0:T(8,128)(2,1)S(1)} collective-permute-done((bf16[1,2,768,128]{3,2,1,0:T(8,128)(2,1)S(1)}, bf16[1,2,768,128]{3,2,1,0:T(8,128)(2,1)S(1)}, u32[]{:S(2)}, u32[]{:S(2)}) %collective-permute-start.5) | collective-permute-done | bytes 393248 | tf_op jit(solution)/shard_map/ppermute | solution.py:314
  53.5 4.2 %collective-permute-done.17.refs_7_ = bf16[1,2,768,128]{3,2,1,0:T(8,128)(2,1)S(1)} collective-permute-done((bf16[1,2,768,128]{3,2,1,0:T(8,128)(2,1)S(1)}, bf16[1,2,768,128]{3,2,1,0:T(8,128)(2,1)S(1)}, u32[]{:S(2)}, u32[]{:S(2)}) %collective-permute-start.17) | collective-permute-done | bytes 393248 | tf_op jit(solution)/shard_map/ppermute | solution.py:314
  57.7 4.3 %collective-permute-done.8.refs_10_ = bf16[1,2,768,128]{3,2,1,0:T(8,128)(2,1)} collective-permute-done((bf16[1,2,768,128]{3,2,1,0:T(8,128)(2,1)}, bf16[1,2,768,128]{3,2,1,0:T(8,128)(2,1)}, u32[]{:S(2)}, u32[]{:S(2)}) %collective-permute-start.8) | collective-permute-done | bytes 393248 | tf_op jit(solution)/shard_map/ppermute | solution.py:321
  63.4 3.3 cut.1
  68.8 71.6 %attend.3.refs_0_ = bf16[12,8,16,128]{3,2,1,0:T(8,128)(2,1)} custom-call(s32[3,2,1,2]{3,2,1,0:T(1,128)} %copy.8.rad, bf16[12,8,16,384]{3,2,1,0:T(8,128)(2,1)} %q.5, bf16[256,384]{1,0:T(8,128)(2,1)} %tk.5, bf16[256,384]{1,0:T(8,128)(2,1)} %tv.5, bf16[1,2,768,128]{3,2,1,0:T(8,128)(2,1)} %bitcast.8, bf16[1,2,768,128]{3,2,1,0:T(8,128)(2,1)} %bitcast.12, ...), custom_call_target="tpu_custom_call" | custom-call | flops 6000000000 | bytes 6000000 | tf_op jit(solution)/shard_map/attend/pallas_call | solution.py:146
  146.4 71.5 %attend.5 = (bf16[6,8,16,128]{3,2,1,0:T(8,128)(2,1)}, bf16[6,8,16,128]{3,2,1,0:T(8,128)(2,1)}) custom-call(s32[3,2,1,2]{3,2,1,0:T(1,128)} %copy.8.rad, bf16[12,8,16,384]{3,2,1,0:T(8,128)(2,1)} %q.5, bf16[256,384]{1,0:T(8,128)(2,1)} %tk.5, bf16[256,384]{1,0:T(8,128)(2,1)} %tv.5, bf16[1,2,768,128]{3,2,1,0:T(8,128)(2,1)} %bitcast.24, ...), custom_call_target="tpu_custom_call" | custom-call | flops 6000000000 | bytes 6000000 | tf_op jit(solution)/shard_map/attend/pallas_call | solution.py:146
  218.5 2.6 collective-permute-start.29
  221.7 71.5 %attend.4.refs_1_ = bf16[12,8,16,128]{3,2,1,0:T(8,128)(2,1)} custom-call(s32[3,2,1,2]{3,2,1,0:T(1,128)} %copy.8.rad, bf16[12,8,16,384]{3,2,1,0:T(8,128)(2,1)} %q.5, bf16[256,384]{1,0:T(8,128)(2,1)} %tk.5, bf16[256,384]{1,0:T(8,128)(2,1)} %tv.5, bf16[1,2,768,128]{3,2,1,0:T(8,128)(2,1)} %bitcast.16, bf16[1,2,768,128]{3,2,1,0:T(8,128)(2,1)} %bitcast.20, ...), custom_call_target="tpu_custom_call" | custom-call | flops 6000000000 | bytes 6000000 | tf_op jit(solution)/shard_map/attend/pallas_call | solution.py:146
  293.7 2.6 collective-permute-start.27
  298.4 2.5 collective-permute-start.31
  302.2 8.4 %collective-permute-done.31.refs_8_ = bf16[6,8,16,128]{3,2,1,0:T(8,128)(2,1)S(1)} collective-permute-done((bf16[6,8,16,128]{3,2,1,0:T(8,128)(2,1)}, bf16[6,8,16,128]{3,2,1,0:T(8,128)(2,1)S(1)}, u32[]{:S(2)}, u32[]{:S(2)}) %collective-permute-start.31) | collective-permute-done | bytes 196640 | tf_op jit(solution)/shard_map/ppermute | solution.py:338
  310.8 4.6 %collective-permute-start.40 = (bf16[6,8,16,128]{3,2,1,0:T(8,128)(2,1)S(1)}, bf16[6,8,16,128]{3,2,1,0:T(8,128)(2,1)}, u32[]{:S(2)}, u32[]{:S(2)}) collective-permute-start(bf16[6,8,16,128]{3,2,1,0:T(8,128)(2,1)S(1)} %copy-done.10), channel_id=1, source_target_pairs={{0,3},{1,0},{2,1},{3,2},{4,7},{5,4},{6,5},{7,6},{8,11},{9,8},{10,9... | collective-permute-start | bytes 589832 | tf_op jit(solution)/shard_map/ppermute | solution.py:338
  316.2 4.3 %project.5 = bf16[6,8,16,384]{3,2,1,0:T(8,128)(2,1)} custom-call(bf16[12,8,16,128]{3,2,1,0:T(8,128)(2,1)} %attend.3.refs_0_, bf16[12,8,16,128]{3,2,1,0:T(8,128)(2,1)} %attend.4.refs_1_, bf16[6,8,16,128]{3,2,1,0:T(8,128)(2,1)} %get-tuple-element.23.refs_2_, bf16[12,8,16,128]{3,2,1,0:T(8,128)(2,1)} %copy-done.4, bf16[12,8,16,128]{3,2,1,0:T(8,128)(2,1)} %copy-done.7, ...), custom_call_target="tpu_custom_call" | custom-call | flops 1000000000 | bytes 4500000 | tf_op jit(solution)/shard_map/project/pallas_call | solution.py:268
  320.6 3.0 collective-permute-start.38
  324.2 4.4 %project.7 = bf16[6,8,16,384]{3,2,1,0:T(8,128)(2,1)} custom-call(bf16[12,8,16,128]{3,2,1,0:T(8,128)(2,1)} %attend.3.refs_0_, bf16[12,8,16,128]{3,2,1,0:T(8,128)(2,1)} %attend.4.refs_1_, bf16[6,8,16,128]{3,2,1,0:T(8,128)(2,1)} %get-tuple-element.28.refs_2_, bf16[12,8,16,128]{3,2,1,0:T(8,128)(2,1)} %copy-done.4, bf16[12,8,16,128]{3,2,1,0:T(8,128)(2,1)} %copy-done.7, ...), custom_call_target="tpu_custom_call" | custom-call | flops 1000000000 | bytes 4500000 | tf_op jit(solution)/shard_map/project/pallas_call | solution.py:268
  330.0 4.6 %project.4 = f32[6,8,16,384]{3,2,1,0:T(8,128)} custom-call(bf16[12,8,16,128]{3,2,1,0:T(8,128)(2,1)} %attend.3.refs_0_, bf16[12,8,16,128]{3,2,1,0:T(8,128)(2,1)} %attend.4.refs_1_, bf16[6,8,16,128]{3,2,1,0:T(8,128)(2,1)} %get-tuple-element.23.refs_2_, bf16[12,8,16,128]{3,2,1,0:T(8,128)(2,1)} %copy-done.4, bf16[12,8,16,128]{3,2,1,0:T(8,128)(2,1)} %copy-done.7, ...), custom_call_target="tpu_custom_call" | custom-call | flops 1000000000 | bytes 4500000 | tf_op jit(solution)/shard_map/project/pallas_call | solution.py:268
  334.6 4.6 %project.6 = f32[6,8,16,384]{3,2,1,0:T(8,128)} custom-call(bf16[12,8,16,128]{3,2,1,0:T(8,128)(2,1)} %attend.3.refs_0_, bf16[12,8,16,128]{3,2,1,0:T(8,128)(2,1)} %attend.4.refs_1_, bf16[6,8,16,128]{3,2,1,0:T(8,128)(2,1)} %get-tuple-element.28.refs_2_, bf16[12,8,16,128]{3,2,1,0:T(8,128)(2,1)} %copy-done.4, bf16[12,8,16,128]{3,2,1,0:T(8,128)(2,1)} %copy-done.7, ...), custom_call_target="tpu_custom_call" | custom-call | flops 1000000000 | bytes 4500000 | tf_op jit(solution)/shard_map/project/pallas_call | solution.py:268
  (154 shorter events, 38.9 us)
Async XLA Ops:
  9.5 20.8 %collective-permute-start.14 = (bf16[2,2,768,128]{3,2,1,0:T(8,128)(2,1)}, bf16[2,2,768,128]{3,2,1,0:T(8,128)(2,1)}, u32[]{:S(2)}, u32[]{:S(2)}) collective-permute-start(bf16[2,2,768,128]{3,2,1,0:T(8,128)(2,1)} %choose.3), channel_id=1, source_target_pairs={{0,64},{32,96},{64,0},{96,32},{1,65},{33,97},{65,1},{97,33},{2,66}... | collective-permute-start | bytes 2359304 | tf_op jit(solution)/shard_map/ppermute | solution.py:320
  14.6 18.4 %collective-permute-start.16 = (bf16[1,2,768,128]{3,2,1,0:T(8,128)(2,1)S(1)}, bf16[1,2,768,128]{3,2,1,0:T(8,128)(2,1)S(1)}, u32[]{:S(2)}, u32[]{:S(2)}) collective-permute-start(bf16[1,2,768,128]{3,2,1,0:T(8,128)(2,1)S(1)} %bitcast.21), channel_id=1, source_target_pairs={{0,8},{8,16},{16,24},{24,0},{1,9},{9,17},{17,25},{25,1},{2,10},{10... | collective-permute-start | bytes 1179656 | tf_op jit(solution)/shard_map/ppermute | solution.py:313
  18.4 19.5 %collective-permute-start.2 = (bf16[1,2,768,128]{3,2,1,0:T(8,128)(2,1)}, bf16[1,2,768,128]{3,2,1,0:T(8,128)(2,1)}, u32[]{:S(2)}, u32[]{:S(2)}) collective-permute-start(bf16[1,2,768,128]{3,2,1,0:T(8,128)(2,1)} %choose.2), channel_id=1, source_target_pairs={{0,64},{32,96},{64,0},{96,32},{1,65},{33,97},{65,1},{97,33},{2,66}... | collective-permute-start | bytes 1179656 | tf_op jit(solution)/shard_map/ppermute | solution.py:320
  30.3 32.3 %collective-permute-start.20 = (bf16[2,2,768,128]{3,2,1,0:T(8,128)(2,1)}, bf16[2,2,768,128]{3,2,1,0:T(8,128)(2,1)}, u32[]{:S(2)}, u32[]{:S(2)}) collective-permute-start(bf16[2,2,768,128]{3,2,1,0:T(8,128)(2,1)} %collective-permute-done.14.refs_4_), channel_id=1, source_target_pairs={{8,0},{16,8},{24,16},{0,24},{32,40},{40,48},{48,56},{56,32},{72,64... | collective-permute-start | bytes 2359304 | tf_op jit(solution)/shard_map/ppermute | solution.py:321
  30.8 22.7 %collective-permute-start.5 = (bf16[1,2,768,128]{3,2,1,0:T(8,128)(2,1)S(1)}, bf16[1,2,768,128]{3,2,1,0:T(8,128)(2,1)S(1)}, u32[]{:S(2)}, u32[]{:S(2)}) collective-permute-start(bf16[1,2,768,128]{3,2,1,0:T(8,128)(2,1)S(1)} %bitcast.9), channel_id=1, source_target_pairs={{8,0},{16,8},{24,16},{0,24},{9,1},{17,9},{25,17},{1,25},{10,2},{18... | collective-permute-start | bytes 1179656 | tf_op jit(solution)/shard_map/ppermute | solution.py:314
  33.0 24.7 %collective-permute-start.17 = (bf16[1,2,768,128]{3,2,1,0:T(8,128)(2,1)S(1)}, bf16[1,2,768,128]{3,2,1,0:T(8,128)(2,1)S(1)}, u32[]{:S(2)}, u32[]{:S(2)}) collective-permute-start(bf16[1,2,768,128]{3,2,1,0:T(8,128)(2,1)S(1)} %bitcast.17), channel_id=1, source_target_pairs={{8,0},{16,8},{24,16},{0,24},{9,1},{17,9},{25,17},{1,25},{10,2},{18... | collective-permute-start | bytes 1179656 | tf_op jit(solution)/shard_map/ppermute | solution.py:314
  37.9 24.1 %collective-permute-start.8 = (bf16[1,2,768,128]{3,2,1,0:T(8,128)(2,1)}, bf16[1,2,768,128]{3,2,1,0:T(8,128)(2,1)}, u32[]{:S(2)}, u32[]{:S(2)}) collective-permute-start(bf16[1,2,768,128]{3,2,1,0:T(8,128)(2,1)} %collective-permute-done.2.refs_4_), channel_id=1, source_target_pairs={{8,0},{16,8},{24,16},{0,24},{32,40},{40,48},{48,56},{56,32},{72,64... | collective-permute-start | bytes 1179656 | tf_op jit(solution)/shard_map/ppermute | solution.py:321
  41.4 20.6 %collective-permute-start.6 = (bf16[1,2,768,128]{3,2,1,0:T(8,128)(2,1)S(1)}, bf16[1,2,768,128]{3,2,1,0:T(8,128)(2,1)S(1)}, u32[]{:S(2)}, u32[]{:S(2)}) collective-permute-start(bf16[1,2,768,128]{3,2,1,0:T(8,128)(2,1)S(1)} %collective-permute-done.4.refs_6_), channel_id=1, source_target_pairs={{0,32},{32,0},{64,96},{96,64},{1,33},{33,1},{65,97},{97,65},{2,34}... | collective-permute-start | bytes 1179656 | tf_op jit(solution)/shard_map/ppermute | solution.py:305
  62.0 83.5 %collective-permute-start.15 = (bf16[2,2,768,128]{3,2,1,0:T(8,128)(2,1)}, bf16[2,2,768,128]{3,2,1,0:T(8,128)(2,1)S(1)}, u32[]{:S(2)}, u32[]{:S(2)}) collective-permute-start(bf16[2,2,768,128]{3,2,1,0:T(8,128)(2,1)} %collective-permute-done.14.refs_4_), channel_id=1, source_target_pairs={{0,32},{32,0},{64,96},{96,64},{1,33},{33,1},{65,97},{97,65},{2,34}... | collective-permute-start | bytes 2359304 | tf_op jit(solution)/shard_map/ppermute | solution.py:305
  62.6 83.0 %collective-permute-start.21 = (bf16[2,2,768,128]{3,2,1,0:T(8,128)(2,1)}, bf16[2,2,768,128]{3,2,1,0:T(8,128)(2,1)}, u32[]{:S(2)}, u32[]{:S(2)}) collective-permute-start(bf16[2,2,768,128]{3,2,1,0:T(8,128)(2,1)} %collective-permute-done.20.refs_10_), channel_id=1, source_target_pairs={{0,32},{32,0},{64,96},{96,64},{1,33},{33,1},{65,97},{97,65},{2,34}... | collective-permute-start | bytes 2359304 | tf_op jit(solution)/shard_map/ppermute | solution.py:305
  66.7 151.1 %collective-permute-start.35 = (bf16[2,384,384]{2,1,0:T(8,128)(2,1)}, bf16[2,384,384]{2,1,0:T(8,128)(2,1)S(1)}, u32[]{:S(2)}, u32[]{:S(2)}) collective-permute-start(bf16[2,384,384]{2,1,0:T(8,128)(2,1)} %get-tuple-element.25), channel_id=1, source_target_pairs={{0,1},{1,2},{2,3},{3,0},{4,5},{5,6},{6,7},{7,4},{8,9},{9,10},{10,1... | collective-permute-start | bytes 1769480 | tf_op jit(solution)/shard_map/ppermute | solution.py:330
  68.3 72.1 %collective-permute-start.24 = (bf16[1,2,768,128]{3,2,1,0:T(8,128)(2,1)}, bf16[1,2,768,128]{3,2,1,0:T(8,128)(2,1)S(1)}, u32[]{:S(2)}, u32[]{:S(2)}) collective-permute-start(bf16[1,2,768,128]{3,2,1,0:T(8,128)(2,1)} %collective-permute-done.22.refs_6_), channel_id=1, source_target_pairs={{0,32},{32,0},{64,96},{96,64},{1,33},{33,1},{65,97},{97,65},{2,34}... | collective-permute-start | bytes 1179656 | tf_op jit(solution)/shard_map/ppermute | solution.py:305
  68.4 74.5 %collective-permute-start.25 = (bf16[1,2,768,128]{3,2,1,0:T(8,128)(2,1)}, bf16[1,2,768,128]{3,2,1,0:T(8,128)(2,1)S(1)}, u32[]{:S(2)}, u32[]{:S(2)}) collective-permute-start(bf16[1,2,768,128]{3,2,1,0:T(8,128)(2,1)} %collective-permute-done.23.refs_7_), channel_id=1, source_target_pairs={{0,32},{32,0},{64,96},{96,64},{1,33},{33,1},{65,97},{97,65},{2,34}... | collective-permute-start | bytes 1179656 | tf_op jit(solution)/shard_map/ppermute | solution.py:305
  141.1 152.0 %collective-permute-start.36 = (bf16[2,384,384]{2,1,0:T(8,128)(2,1)}, bf16[2,384,384]{2,1,0:T(8,128)(2,1)S(1)}, u32[]{:S(2)}, u32[]{:S(2)}) collective-permute-start(bf16[2,384,384]{2,1,0:T(8,128)(2,1)} %get-tuple-element.26), channel_id=1, source_target_pairs={{0,3},{1,0},{2,1},{3,2},{4,7},{5,4},{6,5},{7,6},{8,11},{9,8},{10,9... | collective-permute-start | bytes 1769480 | tf_op jit(solution)/shard_map/ppermute | solution.py:331
  143.7 150.0 %collective-permute-start.37 = (bf16[2,384,384]{2,1,0:T(8,128)(2,1)}, bf16[2,384,384]{2,1,0:T(8,128)(2,1)S(1)}, u32[]{:S(2)}, u32[]{:S(2)}) collective-permute-start(bf16[2,384,384]{2,1,0:T(8,128)(2,1)} %get-tuple-element.27), channel_id=1, source_target_pairs={{0,2},{1,3},{2,0},{3,1},{4,6},{5,7},{6,4},{7,5},{8,10},{9,11},{10,... | collective-permute-start | bytes 1769480 | tf_op jit(solution)/shard_map/ppermute | solution.py:332
  145.5 73.1 %collective-permute-start.18 = (bf16[1,2,768,128]{3,2,1,0:T(8,128)(2,1)S(1)}, bf16[1,2,768,128]{3,2,1,0:T(8,128)(2,1)}, u32[]{:S(2)}, u32[]{:S(2)}) collective-permute-start(bf16[1,2,768,128]{3,2,1,0:T(8,128)(2,1)S(1)} %copy-done.30), channel_id=1, source_target_pairs={{0,32},{32,0},{64,96},{96,64},{1,33},{33,1},{65,97},{97,65},{2,34}... | collective-permute-start | bytes 1179656 | tf_op jit(solution)/shard_map/ppermute | solution.py:305
  145.6 75.6 %collective-permute-start.19 = (bf16[1,2,768,128]{3,2,1,0:T(8,128)(2,1)}, bf16[1,2,768,128]{3,2,1,0:T(8,128)(2,1)}, u32[]{:S(2)}, u32[]{:S(2)}) collective-permute-start(bf16[1,2,768,128]{3,2,1,0:T(8,128)(2,1)} %copy-done.31), channel_id=1, source_target_pairs={{0,32},{32,0},{64,96},{96,64},{1,33},{33,1},{65,97},{97,65},{2,34}... | collective-permute-start | bytes 1179656 | tf_op jit(solution)/shard_map/ppermute | solution.py:305
  217.9 78.4 %collective-permute-start.26 = (bf16[12,8,16,128]{3,2,1,0:T(8,128)(2,1)S(1)}, bf16[12,8,16,128]{3,2,1,0:T(8,128)(2,1)S(1)}, u32[]{:S(2)}, u32[]{:S(2)}) collective-permute-start(bf16[12,8,16,128]{3,2,1,0:T(8,128)(2,1)S(1)} %copy-done.3), channel_id=1, source_target_pairs={{0,1},{1,2},{2,3},{3,0},{4,5},{5,6},{6,7},{7,4},{8,9},{9,10},{10,1... | collective-permute-start | bytes 1179656 | tf_op jit(solution)/shard_map/ppermute | solution.py:337
  218.5 78.4 %collective-permute-start.29 = (bf16[12,8,16,128]{3,2,1,0:T(8,128)(2,1)S(1)}, bf16[12,8,16,128]{3,2,1,0:T(8,128)(2,1)S(1)}, u32[]{:S(2)}, u32[]{:S(2)}) collective-permute-start(bf16[12,8,16,128]{3,2,1,0:T(8,128)(2,1)S(1)} %copy-done.3), channel_id=1, source_target_pairs={{0,3},{1,0},{2,1},{3,2},{4,7},{5,4},{6,5},{7,6},{8,11},{9,8},{10,9... | collective-permute-start | bytes 1179656 | tf_op jit(solution)/shard_map/ppermute | solution.py:338
  221.2 77.3 %collective-permute-start.32 = (bf16[12,8,16,128]{3,2,1,0:T(8,128)(2,1)S(1)}, bf16[12,8,16,128]{3,2,1,0:T(8,128)(2,1)S(1)}, u32[]{:S(2)}, u32[]{:S(2)}) collective-permute-start(bf16[12,8,16,128]{3,2,1,0:T(8,128)(2,1)S(1)} %copy-done.3), channel_id=1, source_target_pairs={{0,2},{1,3},{2,0},{3,1},{4,6},{5,7},{6,4},{7,5},{8,10},{9,11},{10,... | collective-permute-start | bytes 1179656 | tf_op jit(solution)/shard_map/ppermute | solution.py:339
  293.7 21.7 %collective-permute-start.27 = (bf16[12,8,16,128]{3,2,1,0:T(8,128)(2,1)}, bf16[12,8,16,128]{3,2,1,0:T(8,128)(2,1)S(1)}, u32[]{:S(2)}, u32[]{:S(2)}) collective-permute-start(bf16[12,8,16,128]{3,2,1,0:T(8,128)(2,1)} %attend.4.refs_1_), channel_id=1, source_target_pairs={{0,1},{1,2},{2,3},{3,0},{4,5},{5,6},{6,7},{7,4},{8,9},{9,10},{10,1... | collective-permute-start | bytes 1179656 | tf_op jit(solution)/shard_map/ppermute | solution.py:337
  296.3 19.6 %collective-permute-start.30 = (bf16[12,8,16,128]{3,2,1,0:T(8,128)(2,1)}, bf16[12,8,16,128]{3,2,1,0:T(8,128)(2,1)}, u32[]{:S(2)}, u32[]{:S(2)}) collective-permute-start(bf16[12,8,16,128]{3,2,1,0:T(8,128)(2,1)} %attend.4.refs_1_), channel_id=1, source_target_pairs={{0,3},{1,0},{2,1},{3,2},{4,7},{5,4},{6,5},{7,6},{8,11},{9,8},{10,9... | collective-permute-start | bytes 1179656 | tf_op jit(solution)/shard_map/ppermute | solution.py:338
  296.9 19.0 %collective-permute-start.33 = (bf16[12,8,16,128]{3,2,1,0:T(8,128)(2,1)}, bf16[12,8,16,128]{3,2,1,0:T(8,128)(2,1)}, u32[]{:S(2)}, u32[]{:S(2)}) collective-permute-start(bf16[12,8,16,128]{3,2,1,0:T(8,128)(2,1)} %attend.4.refs_1_), channel_id=1, source_target_pairs={{0,2},{1,3},{2,0},{3,1},{4,6},{5,7},{6,4},{7,5},{8,10},{9,11},{10,... | collective-permute-start | bytes 1179656 | tf_op jit(solution)/shard_map/ppermute | solution.py:339
  320.6 18.7 %collective-permute-start.38 = (bf16[6,8,16,384]{3,2,1,0:T(8,128)(2,1)}, bf16[6,8,16,384]{3,2,1,0:T(8,128)(2,1)S(1)}, u32[]{:S(2)}, u32[]{:S(2)}) collective-permute-start(bf16[6,8,16,384]{3,2,1,0:T(8,128)(2,1)} %project.5), channel_id=1, source_target_pairs={{0,4},{1,5},{2,6},{3,7},{4,0},{5,1},{6,2},{7,3},{8,12},{9,13},{10,... | collective-permute-start | bytes 1769480 | tf_op jit(solution)/shard_map/ppermute | solution.py:355
  (57 other events, 830.7 us)
